TPU v7x, 32 devices: a whole 2x2x4 slice. The times are simulated.
32 devices in a mesh: grp: 8 (over y, x, core), shard: 4 (over z).
Axes of the slice: x: 2, y: 2, z: 4, core: 2. Of those that a mesh axis runs over, the one named last changes fastest.
Arguments:
- hidden_states: bfloat16 [16384, 1024], P(('grp', 'shard')), may hold values from -6 to 6
- output_cotangent: bfloat16 [16384, 1024], P(('grp', 'shard')), may hold values from -6 to 6
- first_gain: float32 [1024], P('shard'), may hold values from 0.5 to 1.5
- first_bias: float32 [1024], P('shard'), may hold values from -0.1875 to 0.1875
- second_gain: float32 [1024], P('shard'), may hold values from 0.5 to 1.5
- second_bias: float32 [1024], P('shard'), may hold values from -0.1875 to 0.1875
- triple_weight: float32 [1024, 3072], P('shard'), may hold values from -0.1875 to 0.1875
- triple_bias: float32 [3072], P('shard'), may hold values from -0.1875 to 0.1875
- output_weight: float32 [1024, 1024], P('shard'), may hold values from -0.5 to 0.5
- output_bias: float32 [1024], P('shard'), may hold values from -0.1875 to 0.1875
- expand_weight: float32 [1024, 4096], P('shard'), may hold values from -0.1875 to 0.1875
- expand_bias: float32 [4096], P('shard'), may hold values from -0.1875 to 0.1875
- shrink_weight: float32 [4096, 1024], P('shard'), may hold values from -0.09375 to 0.09375
- shrink_bias: float32 [1024], P('shard'), may hold values from -0.1875 to 0.1875
- first_gain_momentum: float32 [1024], P('shard'), may hold values from -6 to 6
- first_bias_momentum: float32 [1024], P('shard'), may hold values from -6 to 6
- second_gain_momentum: float32 [1024], P('shard'), may hold values from -6 to 6
- second_bias_momentum: float32 [1024], P('shard'), may hold values from -6 to 6
- triple_weight_momentum: float32 [1024, 3072], P('shard'), may hold values from -6 to 6
- triple_bias_momentum: float32 [3072], P('shard'), may hold values from -6 to 6
- output_weight_momentum: float32 [1024, 1024], P('shard'), may hold values from -6 to 6
- output_bias_momentum: float32 [1024], P('shard'), may hold values from -6 to 6
- expand_weight_momentum: float32 [1024, 4096], P('shard'), may hold values from -6 to 6
- expand_bias_momentum: float32 [4096], P('shard'), may hold values from -6 to 6
- shrink_weight_momentum: float32 [4096, 1024], P('shard'), may hold values from -6 to 6
- shrink_bias_momentum: float32 [1024], P('shard'), may hold values from -6 to 6
- first_gain_variance: float32 [1024], P('shard'), may hold values from 163.84 to 3276.8
- first_bias_variance: float32 [1024], P('shard'), may hold values from 1 to 10
- second_gain_variance: float32 [1024], P('shard'), may hold values from 163.84 to 3276.8
- second_bias_variance: float32 [1024], P('shard'), may hold values from 1 to 10
- triple_weight_variance: float32 [1024, 3072], P('shard'), may hold values from 1 to 10
- triple_bias_variance: float32 [3072], P('shard'), may hold values from 1 to 10
- output_weight_variance: float32 [1024, 1024], P('shard'), may hold values from 1 to 10
- output_bias_variance: float32 [1024], P('shard'), may hold values from 1 to 10
- expand_weight_variance: float32 [1024, 4096], P('shard'), may hold values from 1 to 10
- expand_bias_variance: float32 [4096], P('shard'), may hold values from 1 to 10
- shrink_weight_variance: float32 [4096, 1024], P('shard'), may hold values from 1 to 10
- shrink_bias_variance: float32 [1024], P('shard'), may hold values from 1 to 10
Outputs:
- block_output: bfloat16 [16384, 1024], P(('grp', 'shard'))
- input_gradient: bfloat16 [16384, 1024], P(('grp', 'shard'))
- first_gain_gradient: float32 [1024], P('shard')
- first_bias_gradient: float32 [1024], P('shard')
- second_gain_gradient: float32 [1024], P('shard')
- second_bias_gradient: float32 [1024], P('shard')
- triple_weight_gradient: float32 [1024, 3072], P('shard')
- triple_bias_gradient: float32 [3072], P('shard')
- output_weight_gradient: float32 [1024, 1024], P('shard')
- output_bias_gradient: float32 [1024], P('shard')
- expand_weight_gradient: float32 [1024, 4096], P('shard')
- expand_bias_gradient: float32 [4096], P('shard')
- shrink_weight_gradient: float32 [4096, 1024], P('shard')
- shrink_bias_gradient: float32 [1024], P('shard')
- first_gain_change: float32 [1024], P('shard')
- first_bias_updated: float32 [1024], P('shard')
- second_gain_change: float32 [1024], P('shard')
- second_bias_updated: float32 [1024], P('shard')
- triple_weight_updated: float32 [1024, 3072], P('shard')
- triple_bias_updated: float32 [3072], P('shard')
- output_weight_updated: float32 [1024, 1024], P('shard')
- output_bias_updated: float32 [1024], P('shard')
- expand_weight_updated: float32 [1024, 4096], P('shard')
- expand_bias_updated: float32 [4096], P('shard')
- shrink_weight_updated: float32 [4096, 1024], P('shard')
- shrink_bias_updated: float32 [1024], P('shard')
- first_gain_momentum_updated: float32 [1024], P('shard')
- first_bias_momentum_updated: float32 [1024], P('shard')
- second_gain_momentum_updated: float32 [1024], P('shard')
- second_bias_momentum_updated: float32 [1024], P('shard')
- triple_weight_momentum_updated: float32 [1024, 3072], P('shard')
- triple_bias_momentum_updated: float32 [3072], P('shard')
- output_weight_momentum_updated: float32 [1024, 1024], P('shard')
- output_bias_momentum_updated: float32 [1024], P('shard')
- expand_weight_momentum_updated: float32 [1024, 4096], P('shard')
- expand_bias_momentum_updated: float32 [4096], P('shard')
- shrink_weight_momentum_updated: float32 [4096, 1024], P('shard')
- shrink_bias_momentum_updated: float32 [1024], P('shard')
- first_gain_variance_updated: float32 [1024], P('shard')
- first_bias_variance_updated: float32 [1024], P('shard')
- second_gain_variance_updated: float32 [1024], P('shard')
- second_bias_variance_updated: float32 [1024], P('shard')
- triple_weight_variance_updated: float32 [1024, 3072], P('shard')
- triple_bias_variance_updated: float32 [3072], P('shard')
- output_weight_variance_updated: float32 [1024, 1024], P('shard')
- output_bias_variance_updated: float32 [1024], P('shard')
- expand_weight_variance_updated: float32 [1024, 4096], P('shard')
- expand_bias_variance_updated: float32 [4096], P('shard')
- shrink_weight_variance_updated: float32 [4096, 1024], P('shard')
- shrink_bias_variance_updated: float32 [1024], P('shard')
All inputs are finite; a program needn't handle non-finite values.
Results may differ from a plain program's by a relative error of at most 0.006.
The roundings to bfloat16 on the way count: a program that leaves them out, or rounds other values in their place, can miss the bound.
Values may be sent and summed in bfloat16 or wider, within the bound.
A program may use at most 320 MiB of HBM per device.

v0:
```python
import math

import jax
import jax.numpy as jnp
from jax import lax
from jax.experimental import pallas as pl
from jax.experimental.pallas import tpu as pltpu
from jax.sharding import Mesh, PartitionSpec as P

HEAD_DIM = 64
ROTARY = 16
STEP = 10
eps_norm = 1e-05
rope_base = 10000.0
beta_one = 0.9
beta_two = 0.95
learn_rate = 0.01
adam_eps = 1e-08
weight_decay = 0.01

bf16 = jnp.bfloat16
f32 = jnp.float32


def adam_step(weight, gradient, momentum, variance, decayed):
    momentum_new = beta_one * momentum + (1.0 - beta_one) * gradient
    variance_new = beta_two * variance + (1.0 - beta_two) * gradient * gradient
    mean_hat = momentum_new / (1.0 - beta_one**STEP)
    var_hat = variance_new / (1.0 - beta_two**STEP)
    change = mean_hat / (jnp.sqrt(var_hat) + adam_eps)
    if decayed:
        change = change + weight_decay * weight
    delta = -learn_rate * change
    return (weight + delta, delta, momentum_new, variance_new)


def rotary_tables(length):
    position = jnp.arange(length).astype(f32)[:, None]
    half = ROTARY // 2
    inverse_freq = rope_base ** (-(jnp.arange(half).astype(f32) * 2.0 / ROTARY))
    angles = position * inverse_freq[None, :]
    return jnp.cos(angles), jnp.sin(angles)


def rotate(tensor, cosine, sine):
    half = ROTARY // 2
    a, b, rest = tensor[..., :half], tensor[..., half:ROTARY], tensor[..., ROTARY:]
    return jnp.concatenate([a * cosine - b * sine, b * cosine + a * sine, rest], -1)


def dot32(a, b, dims):
    return lax.dot_general(a, b, (dims, ((), ())), preferred_element_type=f32)


MESH = pl.DeviceIdType.MESH
ANY = pl.BlockSpec(memory_space=pl.ANY)
VM = pl.BlockSpec(memory_space=pltpu.VMEM)
ONE = ((1,), (0,))
NT = ((1,), (1,))
TN = ((0,), (0,))


def rows_of(start, size):
    return pl.ds(pl.multiple_of(start, math.gcd(size, 512)), size)


class Links:
    def __init__(self, R, X, S):
        self.R, self.X, self.S = R, X, S
        self.rep = lax.axis_index("rep")
        self.tx = lax.axis_index("tx")
        self.core = lax.axis_index("core")
        self.z = lax.axis_index("shard")

    def at_core(self):
        return {"core": 1 - self.core}

    def at_tx(self):
        return {"tx": 1 - self.tx}

    def at_rep(self, dr):
        return {"rep": lax.rem(self.rep + dr, self.R)}

    def at_z(self, z):
        return {"shard": z}

    def barrier(self, every_plane=False):
        sem = pltpu.get_barrier_semaphore()

        def tell(where):
            pl.semaphore_signal(sem, inc=1, device_id=where, device_id_type=MESH)

        count = 1 + (self.X - 1) + (self.R - 1)
        tell(self.at_core())
        if self.X > 1:
            tell(self.at_tx())
        for dr in range(1, self.R):
            tell(self.at_rep(dr))

        if every_plane:
            for dz in range(1, self.S):
                tell(self.at_z(lax.rem(self.z + dz, self.S)))
            pl.semaphore_wait(sem, count + self.S - 1)
            return

        @pl.when(self.z > 0)
        def _():
            tell(self.at_z(self.z - 1))

        @pl.when(self.z < self.S - 1)
        def _():
            tell(self.at_z(self.z + 1))

        ends = (self.z > 0).astype(jnp.int32) + (self.z < self.S - 1).astype(jnp.int32)
        pl.semaphore_wait(sem, count + ends)


def remote(src, dst, send, recv, where):
    return pltpu.make_async_remote_copy(
        src_ref=src, dst_ref=dst, send_sem=send, recv_sem=recv, device_id=where, device_id_type=MESH
    )


def local(src, dst, sem):
    return pltpu.make_async_copy(src, dst, sem)


class LineGather:
    def __init__(self, links, own, buf, n, zs, zr, ys, yr, split):
        self.k = links
        self.own, self.buf, self.n = own, buf, n
        self.parts = links.R if split else 1
        self.m = n // self.parts
        self.zs, self.zr, self.ys, self.yr = zs, zr, ys, yr

    def block(self, p, r):
        return self.buf.at[rows_of(p * self.n + r * self.m, self.m)]

    def mine(self):
        return self.k.rep if self.parts > 1 else 0

    def hop(self, src, p, step, way):
        to = self.k.z + 1 if way == 0 else self.k.z - 1
        return remote(
            src, self.block(p, self.mine()), self.zs.at[step, way], self.zr.at[p], self.k.at_z(to)
        )

    def across(self, p, dr):
        b = self.block(p, self.k.rep)
        return remote(b, b, self.ys.at[p, dr], self.yr.at[p, self.k.rep], self.k.at_rep(dr))

    def each_way(self, step, fn):
        z, S = self.k.z, self.k.S
        for way in (0, 1):
            p = z - step if way == 0 else z + step
            here = (step <= z) if way == 0 else (z + step <= S - 1)
            on = (z < S - 1) if way == 0 else (z > 0)
            fn(way, p, here, on)

    def start(self):
        mine = self.mine()

        def go(way, p, here, on):
            @pl.when(on)
            def _():
                self.hop(self.own.at[rows_of(mine * self.m, self.m)], p, 0, way).start()

        self.each_way(0, go)

    def event(self, step):
        def go(way, p, here, on):
            @pl.when(here)
            def _():
                b = self.block(p, self.mine())
                self.hop(b, p, step, way).wait_recv()

                @pl.when(on)
                def _():
                    self.hop(b, p, step, way).start()

                if self.parts > 1:
                    for dr in range(1, self.k.R):
                        self.across(p, dr).start()

        self.each_way(step, go)

    def arrived(self):
        if self.parts == 1:
            return
        for p in range(self.k.S):
            @pl.when(p != self.k.z)
            def _():
                for dr in range(1, self.k.R):
                    r = lax.rem(self.k.rep + dr, self.k.R)
                    b = self.block(p, r)
                    remote(b, b, self.ys.at[p, dr], self.yr.at[p, r], self.k.at_rep(dr)).wait_recv()

    def drain(self):
        for step in range(self.k.S):
            def go(way, p, here, on):
                @pl.when(jnp.logical_and(here, on))
                def _():
                    self.hop(self.block(p, self.mine()), p, step, way).wait_send()

                if step > 0 and self.parts > 1:
                    @pl.when(here)
                    def _():
                        for dr in range(1, self.k.R):
                            self.across(p, dr).wait_send()

            self.each_way(step, go)


def layer_norm_rows(xb):
    xf = xb.astype(f32)
    cen = xf - jnp.mean(xf, -1, keepdims=True)
    return cen * lax.rsqrt(jnp.mean(cen * cen, -1, keepdims=True) + eps_norm)


SMALL_ROWS = 24


def small_row(sm, S, first, count):
    return jnp.concatenate(
        [sm[p * SMALL_ROWS + first + j : p * SMALL_ROWS + first + j + 1, :] for p in range(S) for j in range(count)],
        -1,
    )


def attention_kernel(R, X, S, L, D, FT, *refs):
    (x_ref, dy_ref, wt_m, wo_m, we_m, ws_m, sm_ref, rc_i, ra_i, rb_i) = refs[:10]
    (xg, dyg, wt_o, wo_o, we_o, ws_o, vec_o, ctx_o, gt_o, wtl_o, wth_o, wol_o, woh_o, tbg_o) = refs[10:24]
    (
        xs, dys, n1, gt, wtb, wob, smb, q_s, k_s, v_s, gc_s, kT, vT, ctxT, gqT, gk_a, gv_a, wtl, wth, wol, woh, wog,
        rc_ref, ra_ref, rb_ref, wt_w, wo_w, we_w, ws_w, wt_ref, wo_ref, we_ref, ws_ref,
        zs, zr, ys, yr, tok_s, tok_r, loc, cut,
    ) = refs[24:]
    T = 2 * X
    rows = D // S
    DT = S * HEAD_DIM
    links = Links(R, X, S)
    chunks = []
    for c, (own, buf) in enumerate(
        [(sm_ref, smb), (wt_ref, wtb), (wo_ref, wob), (we_ref, we_o), (ws_ref, ws_o)]
    ):
        chunks.append(
            LineGather(links, own, buf, own.shape[0], zs.at[c], zr.at[c], ys.at[c], yr.at[c], c > 0)
        )
    g_sm, g_wt, g_wo, g_we, g_ws = chunks
    lane = lax.broadcasted_iota(jnp.int32, (1, 128), 1)
    rank = links.tx * 2 + links.core
    fs = FT // S
    cuts = [[], [local(wo_m.at[rows_of(rank * HEAD_DIM, HEAD_DIM)], wo_w, cut.at[3 * S])], [],
            [local(ws_m.at[rows_of(rank * fs, fs)], ws_w, cut.at[3 * S + 1])]]
    for j in range(3):
        for p in range(S):
            block = ((j * S + p) * T + rank) // 2
            cuts[0].append(
                local(
                    wt_m.at[:, pl.ds(pl.multiple_of(block * 128, 128), 128)],
                    wt_w.at[:, pl.ds((j * S + p) * 128, 128)],
                    cut.at[j * S + p],
                )
            )
    for p in range(S):
        cuts[2].append(
            local(
                we_m.at[:, pl.ds(pl.multiple_of((p * T + rank) * fs, fs), fs)],
                we_w.at[:, pl.ds(p * fs, fs)],
                cut.at[3 * S + 2 + p],
            )
        )
    for group in cuts:
        for c in group:
            c.start()
    links.barrier()
    for c in cuts[0]:
        c.wait()

    def half_lanes(block, odd):
        val = wt_w[:, block * 128 : (block + 1) * 128]
        return jnp.where(lax.rem(rank, 2) == odd, val, pltpu.roll(val, HEAD_DIM, 1))

    for b in range(3 * S // 2):
        both = jnp.where(lane < HEAD_DIM, half_lanes(2 * b, 0), half_lanes(2 * b + 1, 1))
        wt_ref[:, b * 128 : (b + 1) * 128] = both.astype(bf16)
    cuts[1][0].wait()
    wo_ref[...] = wo_w[...].astype(bf16)

    own_copies = [
        local(x_ref, xs.at[pl.ds(0, L)], loc.at[0]),
        local(dy_ref, dys.at[pl.ds(0, L)], loc.at[1]),
    ]
    own_copies_late = []
    for c, g in enumerate(chunks):
        (own_copies if c < 3 else own_copies_late).append(local(g.own, g.buf.at[rows_of(links.z * g.n, g.n)], loc.at[2 + c]))

    def token_copy(a, slot):
        buf = (xs, dys)[a]
        src = (x_ref, dy_ref)[a]
        if slot == 1:
            return remote(src, buf.at[pl.ds(L, L)], tok_s.at[a, 1], tok_r.at[a, 1], links.at_core())
        if slot == 2:
            return remote(src, buf.at[pl.ds(2 * L, L)], tok_s.at[a, 2], tok_r.at[a, 2], links.at_tx())
        return remote(
            buf.at[pl.ds(2 * L, L)], buf.at[pl.ds(3 * L, L)], tok_s.at[a, 3], tok_r.at[a, 3], links.at_core()
        )

    g_sm.start()
    g_wt.start()
    g_wo.start()
    if X > 1:
        token_copy(0, 2).start()
        token_copy(1, 2).start()
    token_copy(0, 1).start()
    token_copy(1, 1).start()
    for c in own_copies:
        c.start()

    tables = [local(a, b, cut.at[4 * S + 2 + q]) for q, (a, b) in enumerate(((rc_i, rc_ref), (ra_i, ra_ref), (rb_i, rb_ref)))]
    for c in tables:
        c.start()
    for c in cuts[2] + cuts[3]:
        c.wait()
    we_ref[...] = we_w[...].astype(bf16)
    ws_ref[...] = ws_w[...].astype(bf16)
    for c in own_copies_late:
        c.start()
    own_copies[0].wait()
    own_copies[2].wait()
    for step in range(1, S):
        g_sm.event(step)
    per = rows // 128
    vec_o[...] = jnp.zeros_like(vec_o)
    sm = smb[...]
    for j in range(6):
        vec_o[j : j + 1, 0:D] = small_row(sm, S, j * per, per)
    fper = FT // S // 128
    vec_o[8 : 8 + 1, 0:FT] = small_row(sm, S, 6 * per, fper)
    def head_bias(j, p):
        block = j * (D // 128) + (T * p + rank) // 2
        at = (block // (3 * per)) * SMALL_ROWS + 6 * per + fper + lax.rem(block, 3 * per)
        row = smb[pl.ds(at, 1), :]
        return jnp.where(lax.rem(rank, 2) == p % 2, row, pltpu.roll(row, HEAD_DIM, 1))

    for j in range(3):
        for a in range(S // 2):
            both = jnp.where(lane < HEAD_DIM, head_bias(j, 2 * a), head_bias(j, 2 * a + 1))
            vec_o[9 + j : 10 + j, a * 128 : (a + 1) * 128] = both

    def norm_one(i):
        gain, shift = vec_o[0:1, 0:D], vec_o[1:2, 0:D]

        @pl.loop(0, L // 64)
        def _(b):
            at = rows_of(i * L + b * 64, 64)
            n1[at, :] = (layer_norm_rows(xs[at, :]) * gain + shift).astype(bf16)

    norm_one(0)
    g_wt.event(1)
    g_wo.event(1)
    g_we.start()
    for step in range(2, S):
        g_wt.event(step)
        g_wo.event(step)
    g_ws.start()
    own_copies[1].wait()
    own_copies[3].wait()
    own_copies[4].wait()
    for c in tables:
        c.wait()
    g_wt.arrived()
    g_wo.arrived()
    late = [(g, step) for step in range(1, S) for g in (g_we, g_ws)]

    def pump(i, turn):
        for index in range(T):
            at = 2 * (2 * index + turn)
            todo = late[at : at + 2]
            if todo:
                @pl.when(i == index)
                def _():
                    for g, step in todo:
                        g.event(step)

    half = L // 2
    lane_head = lax.broadcasted_iota(jnp.int32, (1, DT), 1) // HEAD_DIM
    key_at = lax.broadcasted_iota(jnp.int32, (half, half), 0)
    query_at = lax.broadcasted_iota(jnp.int32, (half, half), 1)
    causal = key_at <= query_at

    def slot_body(i, carry):
        here = rows_of(i * L, L)
        for j, dst in enumerate((q_s, k_s, v_s)):
            val = dot32(n1[here, :], wtb[:, j * DT : (j + 1) * DT], ONE) + vec_o[9 + j : 10 + j, 0:DT]
            if j < 2:
                val = (
                    val * rc_ref[...]
                    + pltpu.roll(val, DT - 8, 1) * ra_ref[...]
                    + pltpu.roll(val, 8, 1) * rb_ref[...]
                )
            vb = val.astype(bf16)
            if j == 0:
                q_s[...] = vb * bf16(0.125)
            else:
                dst[...] = vb
                (kT if j == 1 else vT)[...] = vb.T
        gc_s[...] = dot32(dys[here, :], wob[...], NT).astype(bf16)
        gk_a[...] = jnp.zeros_like(gk_a)
        gv_a[...] = jnp.zeros_like(gv_a)
        pump(i, 0)

        def head_body(h, c2):
            mine = (lane_head == h).astype(f32).astype(bf16)
            hrows = rows_of(h * HEAD_DIM, HEAD_DIM)
            for b in range(2):
                qs = pl.ds(b * half, half)
                kl = (b + 1) * half
                km = k_s[0:kl, :] * mine
                sT = dot32(km, q_s[qs, :], NT)
                diag = jnp.where(causal, sT[kl - half :], -1e30)
                sT = diag if b == 0 else jnp.concatenate([sT[: kl - half], diag], 0)
                e = jnp.exp(sT - jnp.max(sT, 0, keepdims=True))
                p = e * (1.0 / jnp.sum(e, 0, keepdims=True))
                pb = p.astype(bf16)
                ctxT[hrows, qs] = dot32(vT[hrows, 0:kl], pb, ONE).astype(bf16)
                gv_a[0:kl, :] += dot32(pb, gc_s[qs, :] * mine, ONE)
                gp = dot32(v_s[0:kl, :] * mine, gc_s[qs, :], NT)
                gs = (p * (gp - jnp.sum(p * gp, 0, keepdims=True))).astype(bf16)
                gk_a[0:kl, :] += dot32(gs, q_s[qs, :] * mine, ONE)
                gqT[hrows, qs] = dot32(kT[hrows, 0:kl], gs, ONE) * 0.125
            return c2

        lax.fori_loop(0, S, head_body, 0)
        pump(i, 1)
        for j in range(3):
            if j == 2:
                val = gv_a[...]
            else:
                val = gqT[...].T if j == 0 else gk_a[...]
                val = (
                    val * rc_ref[...]
                    - pltpu.roll(val, DT - 8, 1) * ra_ref[...]
                    - pltpu.roll(val, 8, 1) * rb_ref[...]
                )
            gt[here, j * DT : (j + 1) * DT] = val.astype(bf16)
        ctx_o[:, rows_of(i * L, L)] = ctxT[...]
        grad = dot32(ctxT[...], dys[here, :], ONE)

        @pl.when(i == 0)
        def _():
            wog[...] = grad

        @pl.when(i > 0)
        def _():
            wog[...] += grad

        if X > 1:
            @pl.when(i == 1)
            def _():
                for a in (0, 1):
                    token_copy(a, 2).wait_recv()
                    token_copy(a, 3).start()

        for nxt in range(1, T):
            @pl.when(i + 1 == nxt)
            def _():
                for a in (0, 1):
                    if nxt != 2:
                        token_copy(a, nxt).wait_recv()

        @pl.when(i + 1 < T)
        def _():
            norm_one(i + 1)

        return carry

    lax.fori_loop(0, T, slot_body, 0)
    outs = [
        local(xs, xg, loc.at[0]),
        local(dys, dyg, loc.at[1]),
        local(wtb, wt_o, loc.at[3]),
        local(wob, wo_o, loc.at[4]),
        local(gt, gt_o, loc.at[7]),
    ]
    for o in outs:
        o.start()
    for g, step in late[4 * T :]:
        g.event(step)
    ones = jnp.ones((8, T * L), bf16)
    tbg_o[...] = dot32(ones, gt[...], ONE)

    m = rows // R

    @pl.loop(0, S)
    def _(p):
        grad = dot32(n1[:, pl.ds(pl.multiple_of(p * rows, rows), rows)], gt[...], TN)
        for r in range(R):
            part = grad[r * m : (r + 1) * m]
            wtl[rows_of((r * S + p) * m, m), :] = part.astype(bf16)

            @pl.when(links.rep == r)
            def _():
                wth[rows_of(p * m, m), :] = part

    mo = HEAD_DIM // R
    for p in range(S):
        for r in range(R):
            part = wog[p * HEAD_DIM + r * mo : p * HEAD_DIM + (r + 1) * mo, :]
            wol[(r * S + p) * mo : (r * S + p + 1) * mo, :] = part.astype(bf16)

            @pl.when(links.rep == r)
            def _():
                woh[p * mo : (p + 1) * mo, :] = part

    last = [
        local(wtl, wtl_o, loc.at[8]),
        local(wth, wth_o, loc.at[9]),
        local(wol, wol_o, loc.at[10]),
        local(woh, woh_o, loc.at[11]),
    ]
    for o in last:
        o.start()
    for c in own_copies_late:
        c.wait()
    g_we.arrived()
    g_ws.arrived()
    for g in chunks:
        g.drain()
    for a in (0, 1):
        for slot in range(1, T):
            token_copy(a, slot).wait_send()
    for o in outs + last:
        o.wait()


def attention_phase(R, X, S, x, dy, wt, wo, we, ws, small, tables):
    L, D = x.shape
    T = 2 * X
    DT = S * HEAD_DIM
    FT = we.shape[1] // T
    fs = FT // S
    rows = D // S
    n = T * L
    sds = jax.ShapeDtypeStruct
    dma = pltpu.SemaphoreType.DMA
    outs = [
        sds((n, D), bf16), sds((n, D), bf16), sds((D, 3 * DT), bf16), sds((DT, D), bf16),
        sds((D, FT), bf16), sds((FT, D), bf16), sds((16, max(D, FT)), f32), sds((DT, n), bf16),
        sds((n, 3 * DT), bf16), sds((D, 3 * DT), bf16), sds((D // R, 3 * DT), f32),
        sds((DT, D), bf16), sds((DT // R, D), f32), sds((8, 3 * DT), f32),
    ]
    specs = [ANY] * 6 + [VM, VM] + [ANY] * 5 + [VM]
    vmem = pltpu.VMEM
    scratch = [
        vmem((n, D), bf16), vmem((n, D), bf16), vmem((n, D), bf16), vmem((n, 3 * DT), bf16),
        vmem((D, 3 * DT), bf16), vmem((DT, D), bf16), vmem((S * SMALL_ROWS, 128), f32),
        vmem((L, DT), bf16), vmem((L, DT), bf16), vmem((L, DT), bf16), vmem((L, DT), bf16),
        vmem((DT, L), bf16), vmem((DT, L), bf16), vmem((DT, L), bf16), vmem((DT, L), f32),
        vmem((L, DT), f32), vmem((L, DT), f32), vmem((D, 3 * DT), bf16), vmem((D // R, 3 * DT), f32),
        vmem((DT, D), bf16), vmem((DT // R, D), f32), vmem((DT, D), f32),
        vmem((L, DT), f32), vmem((L, DT), f32), vmem((L, DT), f32),
        vmem((rows, 3 * S * 128), f32), vmem((HEAD_DIM, D), f32), vmem((rows, FT), f32), vmem((fs, D), f32),
        vmem((rows, 3 * DT), bf16), vmem((HEAD_DIM, D), bf16), vmem((rows, FT), bf16), vmem((fs, D), bf16),
        dma((5, S, 2)), dma((5, S)), dma((5, S, R)), dma((5, S, R)), dma((2, 4)), dma((2, 4)), dma((12,)), dma((4 * S + 5,)),
    ]
    body = lambda *refs: attention_kernel(R, X, S, L, D, FT, *refs)
    return pl.pallas_call(
        body,
        name="attention_phase",
        out_shape=outs,
        in_specs=[ANY] * 10,
        out_specs=specs,
        scratch_shapes=scratch,
        compiler_params=pltpu.CompilerParams(
            collective_id=1, has_side_effects=True, vmem_limit_bytes=60 * 1024 * 1024
        ),
    )(x, dy, wt, wo, we, ws, small, *tables)


class GradSum:
    def __init__(self, links, blocks, m, bufs, sems, piece, only=None):
        self.k, self.B, self.m = links, blocks, m
        self.lo, self.keep, self.yr, self.zs, self.zr, self.fin = bufs
        self.sems, self.piece, self.only = sems, piece, only

    def across(self, f, dr):
        size = self.B * self.m
        r = lax.rem(self.k.rep + dr, self.k.R)
        return remote(
            self.lo.at[rows_of((f * self.k.R + r) * size, size)],
            self.yr.at[rows_of((f * (self.k.R - 1) + dr - 1) * size, size)],
            self.sems["ys"].at[f, dr], self.sems["yr"].at[f, dr], self.k.at_rep(dr),
        )

    def send_across(self, f):
        for dr in range(1, self.k.R):
            self.across(f, dr).start()

    def toward(self, f, p):
        b = 0 if self.only else p
        to = self.zr.at[rows_of(((0 if self.only else f) * self.k.S + self.k.z) * self.m, self.m)]
        return remote(
            self.zs.at[rows_of((f * self.B + b) * self.m, self.m)], to,
            self.sems["zs"].at[f, p], self.sems["zr"].at[f, self.k.z], self.k.at_z(p),
        )

    def owners(self, f, fn):
        if self.only:
            @pl.when(f != self.k.z)
            def _():
                fn(f)
        else:
            for dp in range(1, self.k.S):
                fn(lax.rem(self.k.z + dp, self.k.S))

    def if_owner(self, f, fn):
        if self.only:
            pl.when(f == self.k.z)(fn)
        else:
            fn()

    def sum_across(self, f):
        R, m = self.k.R, self.m
        for dr in range(1, R):
            self.across(f, dr).wait_recv()

        for b in range(self.B):
            at = rows_of((f * self.B + b) * m, m)
            total = self.keep[at, :]
            for dr in range(1, R):
                got = rows_of(((f * (R - 1) + dr - 1) * self.B + b) * m, m)
                total = total + self.yr[got, :].astype(f32)
            self.keep[at, :] = total
            self.zs[at, :] = total.astype(bf16)

        self.owners(f, lambda p: self.toward(f, p).start())

    def total(self, f):
        S, m = self.k.S, self.m

        def go():
            g = 0 if self.only else f
            at = rows_of((f * self.B + (0 if self.only else self.k.z)) * m, m)
            total = self.keep[at, :]
            for dp in range(1, S):
                p = lax.rem(self.k.z + dp, S)
                src = self.zr.at[rows_of((g * S + p) * m, m)]
                remote(src, src, self.sems["zs"].at[f, p], self.sems["zr"].at[f, p], self.k.at_z(p)).wait_recv()
                total = total + self.zr[rows_of((g * S + p) * m, m), :].astype(f32)
            fin = rows_of(g * m, m)
            self.fin[fin, :] = total.astype(bf16)
            src = self.fin.at[fin]
            local(src, self.piece(f, self.k.tx, self.k.core, self.k.rep), self.sems["gl"].at[f]).start()
            for c in self.spread(f, src, self.k.tx, self.k.rep, 0):
                c.start()

        self.if_owner(f, go)

    def spread(self, f, src, tx, r, stage):
        dst = self.piece(f, tx, self.k.core, r)
        src = dst if src is None else src
        out = []
        other = 1 if stage == 2 else 0
        out.append(
            remote(src, dst, self.sems["gcs"].at[f, other, r], self.sems["gcr"].at[f, other, r], self.k.at_core())
        )
        if stage < 2 and self.k.X > 1:
            out.append(remote(src, dst, self.sems["gxs"].at[f, r], self.sems["gxr"].at[f, r], self.k.at_tx()))
        if stage == 0:
            for dr in range(1, self.k.R):
                out.append(remote(src, dst, self.sems["gys"].at[f, dr], self.sems["gyr"].at[f, r], self.k.at_rep(dr)))
        return out

    def replicas(self, fn):
        for dr in range(1, self.k.R):
            fn(dr, lax.rem(self.k.rep + dr, self.k.R))

    def forward_rep(self, f):
        def go():
            def one(dr, r):
                b = self.piece(f, self.k.tx, self.k.core, r)
                remote(b, b, self.sems["gys"].at[f, dr], self.sems["gyr"].at[f, r], self.k.at_rep(dr)).wait_recv()
                for c in self.spread(f, None, self.k.tx, r, 1):
                    c.start()

            self.replicas(one)

        self.if_owner(f, go)

    def forward_tx(self, f):
        if self.k.X == 1:
            return

        def go():
            for r in range(self.k.R):
                b = self.piece(f, 1 - self.k.tx, self.k.core, r)
                remote(b, b, self.sems["gxs"].at[f, r], self.sems["gxr"].at[f, r], self.k.at_tx()).wait_recv()
                for c in self.spread(f, None, 1 - self.k.tx, r, 2):
                    c.start()

        self.if_owner(f, go)

    def finish(self, f):
        for dr in range(1, self.k.R):
            self.across(f, dr).wait_send()
        self.owners(f, lambda p: self.toward(f, p).wait_send())

        def go():
            src = self.fin.at[rows_of((0 if self.only else f) * self.m, self.m)]
            local(src, self.piece(f, self.k.tx, self.k.core, self.k.rep), self.sems["gl"].at[f]).wait()
            for c in self.spread(f, src, self.k.tx, self.k.rep, 0):
                c.wait_send()
            self.replicas(lambda dr, r: [c.wait_send() for c in self.spread(f, None, self.k.tx, r, 1)])
            for other in range(self.k.X):
                tx = self.k.tx if other == 0 else 1 - self.k.tx
                for r in range(self.k.R):
                    if other == 1:
                        for c in self.spread(f, None, tx, r, 2):
                            c.wait_send()
                    b = self.piece(f, tx, 1 - self.k.core, r)
                    remote(
                        b, b, self.sems["gcs"].at[f, other, r], self.sems["gcr"].at[f, other, r], self.k.at_core()
                    ).wait_recv()

        self.if_owner(f, go)


SEM_NAMES = ("ys", "yr", "zs", "zr", "gl", "gcs", "gcr", "gxs", "gxr", "gys", "gyr")


def grad_sems(count, R, X, S):
    dma = pltpu.SemaphoreType.DMA
    return [
        dma((count, R)), dma((count, R)), dma((count, S)), dma((count, S)), dma((count,)),
        dma((count, 2, R)), dma((count, 2, R)), dma((count, R)), dma((count, R)), dma((count, R)), dma((count, R)),
    ]


def feed_kernel(R, X, S, L, D, FT, *refs):
    (xg, dyg, wt_f, wo_f, we_f, ws_f, vec, ctx_i, gt_i, wtl, wth, wol, woh, tbg) = refs[:14]
    (out_o, ing_o, g_wt, g_wo, g_we, g_ws, v_o) = refs[14:21]
    rest = list(refs[21:])
    take = lambda count: [rest.pop(0) for _ in range(count)]
    (xb, dyb, n2b, actb, ghb, web, wsb, wob, ctb) = take(9)
    wt_bufs, wo_bufs, we_bufs, ws_bufs = take(5), take(5), take(6), take(6)
    (send_b, out_r, dx_r, xs_b, out_x, dx_x, vsum, vrecv) = take(8)
    sem_sets = [dict(zip(SEM_NAMES, take(len(SEM_NAMES)))) for _ in range(4)]
    (loc, tok, v_s, v_r, dxk) = take(5)
    T = 2 * X
    n = T * L
    rows = D // S
    DT = S * HEAD_DIM
    fs = FT // S
    k = Links(R, X, S)
    k.barrier(every_plane=True)
    rank = lambda tx, core: tx * 2 + core
    mt, mo, me, ms = rows // R, HEAD_DIM // R, rows // R, fs // R
    u_wt = GradSum(k, S, mt, [wtl] + wt_bufs, sem_sets[0],
                   lambda f, tx, c, r: g_wt.at[rows_of(rank(tx, c) * rows + r * mt, mt)])
    u_wo = GradSum(k, S, mo, [wol] + wo_bufs, sem_sets[1],
                   lambda f, tx, c, r: g_wo.at[rows_of(rank(tx, c) * HEAD_DIM + r * mo, mo)])
    u_we = GradSum(k, S, me, we_bufs, sem_sets[2],
                   lambda f, tx, c, r: g_we.at[rows_of(r * me, me), rows_of((f * T + rank(tx, c)) * fs, fs)])
    u_ws = GradSum(k, 1, ms, ws_bufs, sem_sets[3],
                   lambda f, tx, c, r: g_ws.at[rows_of(rank(tx, c) * fs + r * ms, ms)], only=True)
    first = (u_wt, u_wo)
    for u in first:
        u.send_across(0)

    def load_x(i, place):
        return local(xg.at[rows_of(i * L, L)], xb.at[pl.ds(place * L, L)], loc.at[place])

    load_x(0, 0).start()
    loads = [
        local(we_f, web, loc.at[2]), local(dyg, dyb, loc.at[3]), local(ws_f, wsb, loc.at[4]),
        local(wo_f, wob, loc.at[5]), local(ctx_i, ctb, loc.at[6]),
        local(wth, wt_bufs[0], loc.at[7]), local(woh, wo_bufs[0], loc.at[8]),
    ]
    for c in loads:
        c.start()

    gain1, gain2, shift2 = vec[0:1, 0:D], vec[2:3, 0:D], vec[3:4, 0:D]

    def norm_two(i, place):
        @pl.loop(0, L // 64)
        def _(b):
            n2b[rows_of(i * L + b * 64, 64), :] = (
                layer_norm_rows(xb[pl.ds(pl.multiple_of(place * L + b * 64, 64), 64), :]) * gain2 + shift2
            ).astype(bf16)

    for i in range(T):
        load_x(i, i % 2).wait()
        if i + 1 < T:
            load_x(i + 1, (i + 1) % 2).start()
        norm_two(i, i % 2)
    load_x(1, 0).start()
    for c in loads[:3]:
        c.wait()

    def hidden_body(it, carry):
        i, f = it // S, lax.rem(it, S)
        here, cols = rows_of(i * L, L), pl.ds(pl.multiple_of(f * fs, fs), fs)
        h = dot32(n2b[here, :], web[:, cols], ONE) + vec[8:9, cols]
        cdf = 0.5 * (1.0 + lax.erf(h * math.sqrt(0.5)))
        actb[here, cols] = (h * cdf).astype(bf16)
        slope = cdf + h * (jnp.exp(-0.5 * h * h) * (1.0 / math.sqrt(2.0 * math.pi)))
        ghb[here, cols] = (dot32(dyb[here, :], wsb[cols, :], NT) * slope).astype(bf16)
        return carry

    lax.fori_loop(0, T * S, hidden_body, 0)
    loads[3].wait()
    loads[4].wait()
    half = L // 2

    def feed_rows(i, b):
        at = i * L + b * half
        return dot32(actb[at : at + half, :], wsb[...], ONE) + dot32(ctb[:, at : at + half], wob[...], TN)

    def to_core(which, j):
        land = (out_r, dx_r)[which]
        return remote(
            send_b.at[pl.ds(j * L, L)], land.at[pl.ds(j * L, L)],
            tok.at[which, 0, j], tok.at[which, 1, j], k.at_core(),
        )

    def to_tx(which):
        return remote(
            xs_b.at[pl.ds(which * L, L)], (out_x, dx_x)[which], tok.at[which, 2, 0], tok.at[which, 2, 1], k.at_tx()
        )

    for j in range(X):
        for b in range(2):
            at = j * L + b * half
            send_b[at : at + half, :] = feed_rows(2 * j + 1, b).astype(bf16)
        to_core(0, j).start()
    if X > 1:
        to_core(0, 1).wait_recv()
        for b in range(2):
            got = out_r[L + b * half : L + (b + 1) * half, :].astype(f32)
            xs_b[b * half : (b + 1) * half, :] = (feed_rows(2, b) + got).astype(bf16)
        to_tx(0).start()

    for b in range(2):
        dxk[b * half : (b + 1) * half, :] = feed_rows(0, b)

    side = D // DT
    thirds = [wsb.at[pl.ds((j // side) * D, D), pl.ds((j % side) * DT, DT)] for j in range(3)]
    load_wt = [local(wt_f.at[:, pl.ds(j * DT, DT)], thirds[j], loc.at[(9, 11, 12)[j]]) for j in range(3)]
    for c in load_wt:
        c.start()

    def triple_back(at):
        total = None
        for j in range(0, 3, side):
            wide = min(side, 3 - j)
            part = dot32(
                actb[at, j * DT : (j + wide) * DT], wsb[(j // side) * D : (j // side + 1) * D, 0 : wide * DT], NT
            )
            total = part if total is None else total + part
        return total

    def store_grad(u, f, block, grad):
        for r in range(R):
            part = grad[r * u.m : (r + 1) * u.m]
            u.lo[rows_of(((f * R + r) * u.B + block) * u.m, u.m), :] = part.astype(bf16)

            @pl.when(k.rep == r)
            def _():
                u.keep[rows_of((f * u.B + block) * u.m, u.m), :] = part

    loads[5].wait()
    loads[6].wait()

    def chunk_body(f, carry):
        cols = pl.ds(pl.multiple_of(f * fs, fs), fs)
        store_grad(u_ws, f, 0, dot32(actb[:, cols], dyb[...], TN))
        u_ws.send_across(f)

        def block_body(p, c2):
            grad = dot32(n2b[:, pl.ds(pl.multiple_of(p * rows, rows), rows)], ghb[:, cols], TN)
            store_grad(u_we, f, p, grad)
            return c2

        lax.fori_loop(0, S, block_body, 0)
        u_we.send_across(f)

        @pl.when(f == 0)
        def _():
            for u in first:
                u.sum_across(0)

        return carry

    lax.fori_loop(0, S, chunk_body, 0)
    gtb = actb.at[:, pl.ds(0, 3 * DT)]
    load_gt = local(gt_i, gtb, loc.at[10])
    load_gt.start()
    for j in range(X):
        to_core(0, j).wait_send()
    load_gt.wait()
    for c in load_wt:
        c.wait()

    def pair(step, f):
        for u in (u_we, u_ws):
            getattr(u, step)(f)

    vsum[...] = jnp.zeros_like(vsum)

    def slot_grad(i, place, finish):
        for b in range(2):
            at = pl.ds(i * L + b * half, half)
            xhat = layer_norm_rows(xb[place * L + b * half : place * L + (b + 1) * half, :])
            g1 = triple_back(at)
            vsum[0:1, 0:D] += jnp.sum(g1 * xhat, 0, keepdims=True)
            vsum[1:2, 0:D] += jnp.sum(g1, 0, keepdims=True)
            g2 = dot32(ghb[at, :], web[...], NT)
            vsum[2:3, 0:D] += jnp.sum(g2 * xhat, 0, keepdims=True)
            vsum[3:4, 0:D] += jnp.sum(g2, 0, keepdims=True)
            finish(b, g1 * gain1 + g2 * gain2, xhat)

    order = [2 * j + 1 for j in range(X)] + ([2] if X > 1 else []) + [0]
    events = [("sum_across", f) for f in range(S)]
    for turn, i in enumerate(order):
        place = turn % 2
        load_x(i, place).wait()
        if turn + 1 < T:
            load_x(order[turn + 1], 1 - place).start()
        if i % 2 == 1:
            j = i // 2

            def finish(b, val, xhat):
                at = j * L + b * half
                send_b[at : at + half, :] = val.astype(bf16)

            slot_grad(i, place, finish)
            to_core(1, j).start()
        elif i == 2:
            to_core(1, 1).wait_recv()

            def finish(b, val, xhat):
                got = dx_r[L + b * half : L + (b + 1) * half, :].astype(f32)
                xs_b[L + b * half : L + (b + 1) * half, :] = (val + got).astype(bf16)

            slot_grad(2, place, finish)
            to_tx(1).start()
            pair("sum_across", 0)
            for u in first:
                u.total(0)
        else:
            to_core(0, 0).wait_recv()
            to_core(1, 0).wait_recv()
            if X > 1:
                to_tx(0).wait_recv()
            for j in range(X):
                to_core(1, j).wait_send()
            for b in range(2):
                rows_b = slice(b * half, (b + 1) * half)
                total = dxk[rows_b, :] + out_r[rows_b, :].astype(f32)
                if X > 1:
                    total = total + out_x[rows_b, :].astype(f32)
                total = total + xb[place * L + b * half : place * L + (b + 1) * half, :].astype(f32)
                send_b[rows_b, :] = (total + (vec[4:5, 0:D] + vec[5:6, 0:D])).astype(bf16)
            save_out = local(send_b.at[pl.ds(0, L)], out_o, loc.at[2])
            save_out.start()

            def finish(b, val, xhat):
                rows_b = slice(b * half, (b + 1) * half)
                dxk[rows_b, :] = val + dx_r[rows_b, :].astype(f32)

            slot_grad(0, place, finish)
            place0 = place
    ones = jnp.ones((8, L), bf16)
    vsum[4:5, 0:D] = dot32(ones, dyb[0:L, :], ONE)[0:1]
    mine = rank(k.tx, k.core)
    eb = dot32(jnp.ones((8, n), bf16), ghb[...], ONE)[0:1]
    for t in range(T):
        @pl.when(mine == t)
        def _():
            vsum[5 + t : 6 + t, 0 : 3 * DT] = tbg[0:1, :]
            vsum[5 + T + t : 6 + T + t, 0:FT] = eb

    def exchange(stage, copies):
        for c in copies:
            c.start()
        for c in copies:
            c.wait()
        for q in range(len(copies)):
            vsum[...] += vrecv[stage + q]

    at_stage = 0
    exchange(0, [remote(vsum, vrecv.at[0], v_s.at[0], v_r.at[0], k.at_core())])
    at_stage = 1
    if X > 1:
        exchange(1, [remote(vsum, vrecv.at[1], v_s.at[1], v_r.at[1], k.at_tx())])
        at_stage = 2
    rep_copies = [
        remote(vsum, vrecv.at[at_stage + dr - 1], v_s.at[at_stage + dr - 1], v_r.at[at_stage + dr - 1], k.at_rep(dr))
        for dr in range(1, R)
    ]
    exchange(at_stage, rep_copies)
    at_stage += R - 1
    pair("sum_across", 1)
    for u in first:
        u.forward_rep(0)
    z_copies = [
        remote(
            vsum, vrecv.at[at_stage + dz - 1], v_s.at[at_stage + dz - 1], v_r.at[at_stage + dz - 1],
            k.at_z(lax.rem(k.z + dz, S)),
        )
        for dz in range(1, S)
    ]
    for c in z_copies:
        c.start()
    pair("total", 0)
    for f in range(2, S):
        pair("sum_across", f)
        if f == 2:
            for u in first:
                u.forward_tx(0)
        pair("total", f - 1)
        pair("forward_rep", f - 2)
        if f > 2:
            pair("forward_tx", f - 3)
    for c in z_copies:
        c.wait()
    total = vsum[...]
    for q in range(S - 1):
        total = total + vrecv[at_stage + q]
    v_o[...] = total
    if X > 1:
        to_tx(1).wait_recv()
    for b in range(2):
        rows_b = slice(b * half, (b + 1) * half)
        dx = dxk[rows_b, :]
        if X > 1:
            dx = dx + dx_x[rows_b, :].astype(f32)
        xf = xb[place0 * L + b * half : place0 * L + (b + 1) * half, :].astype(f32)
        cen = xf - jnp.mean(xf, -1, keepdims=True)
        rstd = lax.rsqrt(jnp.mean(cen * cen, -1, keepdims=True) + eps_norm)
        xhat = cen * rstd
        back = dx - jnp.mean(dx, -1, keepdims=True) - xhat * jnp.mean(dx * xhat, -1, keepdims=True)
        send_b[L + b * half : L + (b + 1) * half, :] = (dyb[rows_b, :].astype(f32) + rstd * back).astype(bf16)
    save_ing = local(send_b.at[pl.ds(L, L)], ing_o, loc.at[3])
    save_ing.start()
    pair("total", S - 1)
    pair("forward_rep", S - 2)
    pair("forward_tx", S - 3)
    pair("forward_rep", S - 1)
    pair("forward_tx", S - 2)
    pair("forward_tx", S - 1)
    for u in first:
        u.finish(0)
    for f in range(S):
        pair("finish", f)
    if X > 1:
        to_tx(0).wait_send()
        to_tx(1).wait_send()
    save_out.wait()
    save_ing.wait()


def feed_phase(R, X, S, F, xg, dyg, wt_f, wo_f, we_f, ws_f, vecs, ctxT, gt, wtl, wth, wol, woh, tbg):
    T = 2 * X
    n, D = xg.shape
    L = n // T
    DT = S * HEAD_DIM
    FT = we_f.shape[1]
    fs = FT // S
    rows = D // S
    mt, mo, me, ms = rows // R, HEAD_DIM // R, rows // R, fs // R
    W = max(D, 3 * DT, FT)
    sds = jax.ShapeDtypeStruct
    vmem = pltpu.VMEM
    dma = pltpu.SemaphoreType.DMA
    outs = [
        sds((L, D), bf16), sds((L, D), bf16), sds((T * rows, 3 * DT), bf16), sds((rows, D), bf16),
        sds((rows, F), bf16), sds((F // S, D), bf16), sds((16, W), f32),
    ]

    def bufs(count, B, m, cols, lo, landing):
        made = [vmem((count * R * B * m, cols), bf16)] if lo else []
        return made + [
            vmem((count * B * m, cols), f32), vmem((count * (R - 1) * B * m, cols), bf16),
            vmem((count * B * m, cols), bf16), vmem((landing * S * m, cols), bf16), vmem((landing * m, cols), bf16),
        ]

    scratch = [
        vmem((2 * L, D), bf16), vmem((n, D), bf16), vmem((n, D), bf16), vmem((n, FT), bf16), vmem((n, FT), bf16),
        vmem((D, FT), bf16), vmem((FT, D), bf16), vmem((DT, D), bf16),
        vmem((DT, n), bf16),
    ]
    scratch += bufs(1, S, mt, 3 * DT, False, 1) + bufs(1, S, mo, D, False, 1)
    scratch += bufs(S, S, me, fs, True, S) + bufs(S, 1, ms, D, True, 1)
    scratch += [
        vmem((2 * L, D), bf16), vmem((X * L, D), bf16), vmem((X * L, D), bf16), vmem((2 * L, D), bf16),
        vmem((L, D), bf16), vmem((L, D), bf16), vmem((16, W), f32), vmem((2 + R - 1 + S - 1, 16, W), f32),
    ]
    for count in (1, 1, S, S):
        scratch += grad_sems(count, R, X, S)
    scratch += [dma((13,)), dma((2, 3, 2)), dma((2 + R - 1 + S - 1,)), dma((2 + R - 1 + S - 1,)), vmem((L, D), f32)]
    body = lambda *refs: feed_kernel(R, X, S, L, D, FT, *refs)
    return pl.pallas_call(
        body,
        name="feed_phase",
        out_shape=outs,
        in_specs=[ANY] * 6 + [VM] + [ANY] * 6 + [VM],
        out_specs=[ANY] * 6 + [VM],
        scratch_shapes=scratch,
        compiler_params=pltpu.CompilerParams(
            collective_id=2, has_side_effects=True, vmem_limit_bytes=67_000_000
        ),
    )(xg, dyg, wt_f, wo_f, we_f, ws_f, vecs, ctxT, gt, wtl, wth, wol, woh, tbg)


def adam_kernel(S, T, heads, *refs):
    g_ref, w_ref, m_ref, v_ref, g_o, w_o, m_o, v_o = refs

    def one(at, g):
        new_w, _, new_m, new_v = adam_step(w_ref[:, at], g, m_ref[:, at], v_ref[:, at], True)
        g_o[:, at] = g
        w_o[:, at] = new_w
        m_o[:, at] = new_m
        v_o[:, at] = new_v

    if not heads:
        one(slice(None), g_ref[...].astype(f32))
        return
    lane = lax.broadcasted_iota(jnp.int32, (1, 128), 1)
    DT = S * HEAD_DIM
    for j in range(3):
        for p in range(S):
            src = j * DT + (p // 2) * 128
            for u in range(T // 2):
                low = g_ref[2 * u, :, src : src + 128].astype(f32)
                high = g_ref[2 * u + 1, :, src : src + 128].astype(f32)
                if p % 2 == 1:
                    low = pltpu.roll(low, HEAD_DIM, 1)
                else:
                    high = pltpu.roll(high, HEAD_DIM, 1)
                to = ((j * S + p) * T + 2 * u) * HEAD_DIM
                one(slice(to, to + 128), jnp.where(lane < HEAD_DIM, low, high))


def adam_matrix(S, T, g, w, m, v, heads, rows_each):
    n, cols = w.shape
    spec = pl.BlockSpec((rows_each, cols), lambda i: (i, 0))
    g_spec = pl.BlockSpec((T, rows_each, g.shape[-1]), lambda i: (0, i, 0)) if heads else spec
    return pl.pallas_call(
        lambda *refs: adam_kernel(S, T, heads, *refs),
        name="adam_matrix",
        grid=(n // rows_each,),
        out_shape=[jax.ShapeDtypeStruct((n, cols), f32)] * 4,
        in_specs=[g_spec, spec, spec, spec],
        out_specs=[spec] * 4,
        compiler_params=pltpu.CompilerParams(vmem_limit_bytes=40 * 1024 * 1024),
    )(g, w, m, v)


TP = ("tx", "core")


def make_step(R, X, S):
    T = 2 * X

    def step(*args):
        x, dy = args[0], args[1]
        masters, momenta, variances = args[2:14], args[14:26], args[26:38]
        L, D = x.shape
        H = D // HEAD_DIM
        t = lax.axis_index(TP)
        z = lax.axis_index("shard")
        rep = lax.axis_index("rep")
        wt, wo, we, ws = masters[4], masters[6], masters[8], masters[10]
        rows = wt.shape[0]
        F = we.shape[1]
        fs = F // S // T
        HT = H // T

        eb_own = lax.dynamic_slice_in_dim(masters[9], t * fs, fs, 0)
        packed = [masters[i] for i in (0, 1, 2, 3, 7, 11)] + [eb_own, masters[5]]
        width = sum(v.shape[0] for v in packed)
        packed.append(jnp.zeros((SMALL_ROWS * 128 - width,), f32))
        small = lax.reduce_precision(jnp.concatenate(packed).reshape(SMALL_ROWS, 128), 8, 7)

        cosine, sine = rotary_tables(L)
        zero, one = jnp.zeros((L, 8), f32), jnp.ones((L, HEAD_DIM - 16), f32)
        pad = jnp.zeros((L, HEAD_DIM - 16), f32)
        tables = (
            jnp.tile(jnp.concatenate([cosine, cosine, one], 1), (1, S)),
            jnp.tile(jnp.concatenate([-sine, zero, pad], 1), (1, S)),
            jnp.tile(jnp.concatenate([zero, sine, pad], 1), (1, S)),
        )
        passed = attention_phase(R, X, S, x, dy, wt, wo, we, ws, small, tables)
        out, in_grad, wt_s, wo_s, we_s, ws_s, vec = feed_phase(R, X, S, F, *passed)
        wt_s = wt_s.reshape(T, rows, -1)
        DT, FT = S * HEAD_DIM, F // T
        tb_g = vec[5 : 5 + T, : 3 * DT].reshape(T, 3, S, HEAD_DIM).transpose(1, 2, 0, 3).reshape(-1)
        eb_g = vec[5 + T : 5 + 2 * T, :FT].reshape(T, S, fs).transpose(1, 0, 2).reshape(-1)

        def own(v):
            return lax.dynamic_slice_in_dim(v, z * (v.shape[0] // S), v.shape[0] // S, 0)

        vown = [own(vec[i, :D]) for i in range(5)] + [own(tb_g), own(eb_g)]
        done = {}
        for i, g, each in ((4, wt_s, 64), (6, wo_s, 128), (8, we_s, 64), (10, ws_s, 256)):
            each = min(each, g.shape[-2])
            done[i] = adam_matrix(S, T, g, masters[i], momenta[i], variances[i], i == 4, each)
        summed = [
            vown[0], vown[1], vown[2], vown[3], None, vown[5], None, vown[4], None, vown[6], None, vown[4],
        ]
        updated, ones, twos = [], [], []
        for i in range(12):
            if i in done:
                summed[i] = done[i][0]
                for kept, val in zip((updated, ones, twos), done[i][1:]):
                    kept.append(val)
                continue
            new_weight, delta, m_new, v_new = adam_step(
                masters[i], summed[i], momenta[i], variances[i], i in (4, 6, 8, 10)
            )
            updated.append(delta if i in (0, 2) else new_weight)
            ones.append(m_new)
            twos.append(v_new)
        return (out, in_grad, *summed, *updated, *ones, *twos)

    return step


def solution(mesh):
    G, S = mesh.shape["grp"], mesh.shape["shard"]
    X = 2 if S <= 4 else 1
    R = G // (2 * X)
    full = Mesh(mesh.devices.reshape(R, X, 2, S), ("rep", "tx", "core", "shard"))
    tok = P(("rep", "tx", "core", "shard"), None)
    vecs, mats = P("shard"), P("shard", None)
    group = tuple(mats if i in (4, 6, 8, 10) else vecs for i in range(12))
    return jax.shard_map(
        make_step(R, X, S),
        mesh=full,
        in_specs=(tok, tok) + group * 3,
        out_specs=(tok, tok) + group * 4,
        check_vma=False,
    )
```

profile of v0, /device:TPU:27, one launch (start us, length us, event | category | flops | bytes accessed | tf_op | source)
XLA Modules:
  0.0 315.0 jit_solution(1548523271999791282)
XLA Ops:
  0.7 0.7 constant_dynamic-update-slice_fusion.8
  1.4 0.7 constant_dynamic-update-slice_fusion.7
  2.1 0.7 constant_dynamic-update-slice_fusion.6
  2.8 0.7 constant_dynamic-update-slice_fusion.5
  3.5 0.7 constant_dynamic-update-slice_fusion.4
  4.1 0.7 constant_dynamic-update-slice_fusion.3
  4.8 0.8 constant_dynamic-update-slice_fusion.2
  5.6 0.7 constant_dynamic-update-slice_fusion.1
  6.3 0.6 reduce-precision_bitcast_fusion.refs_6_
  6.9 0.1 multiply_sine_fusion
  7.4 1.0 copy.88.refs_7_
  8.5 1.0 copy.89.refs_8_
  9.5 1.0 copy.90.refs_9_
  10.5 93.9 %attention_phase.1 = (bf16[2048,1024]{1,0:T(8,128)(2,1)}, bf16[2048,1024]{1,0:T(8,128)(2,1)}, bf16[1024,768]{1,0:T(8,128)(2,1)}, bf16[256,1024]{1,0:T(8,128)(2,1...) custom-call(bf16[512,1024]{1,0:T(8,128)(2,1)} %refs_0_.1, ...), custom_call_target="tpu_custom_call" | custom-call | tf_op jit(solution)/shard_map/attention_phase/pallas_call | solution.py:568
  104.5 164.3 %feed_phase.1 = (bf16[512,1024]{1,0:T(8,128)(2,1)}, bf16[512,1024]{1,0:T(8,128)(2,1)}, bf16[1024,768]{1,0:T(8,128)(2,1)}, bf16[256,1024]{1,0:T(8,128)(2,1)}, bf1...) custom-call(bf16[2048,1024]{1,0:T(8,128)(2,1)} %get-tuple-element.87.refs_0_, ...), custom_call_target="tpu_custom_call" | custom-call | tf_op jit(solution)/shard_map/feed_phase/pallas_call | solution.py:1104
  268.8 2.2 copy-done
  270.9 2.2 copy-done.3
  273.1 1.6 copy-done.9
  274.7 12.3 %adam_matrix.6 = (f32[256,4096]{1,0:T(8,128)}, f32[256,4096]{1,0:T(8,128)}, f32[256,4096]{1,0:T(8,128)}, f32[256,4096]{1,0:T(8,128)}) custom-call(bf16[256,4096]{1,0:T(8,128)(2,1)S(1)} %copy-done.9, f32[256,4096]{1,0:T(8,128)S(1)} %copy-done, f32[256,4096]{1,0:T(8,128)S(1)} %copy-done.3, f32[256,4096]{1,0:T(8,128)} %refs_3_.8), custom_call_target="tpu_custom_call" | custom-call | tf_op jit(solution)/shard_map/adam_matrix/pallas_call | solution.py:1150
  287.1 11.7 %adam_matrix.7 = (f32[1024,1024]{1,0:T(8,128)}, f32[1024,1024]{1,0:T(8,128)}, f32[1024,1024]{1,0:T(8,128)}, f32[1024,1024]{1,0:T(8,128)}) custom-call(bf16[1024,1024]{1,0:T(8,128)(2,1)S(1)} %copy-done.8, f32[1024,1024]{1,0:T(8,128)S(1)} %copy-done.1, f32[1024,1024]{1,0:T(8,128)S(1)} %copy-done.4, f32[1024,1024]{1,0:T(8,128)} %refs_3_.9), custom_call_target="tpu_custom_call" | custom-call | tf_op jit(solution)/shard_map/adam_matrix/pallas_call | solution.py:1150
  299.2 5.8 %adam_matrix.4 = (f32[256,3072]{1,0:T(8,128)}, f32[256,3072]{1,0:T(8,128)}, f32[256,3072]{1,0:T(8,128)}, f32[256,3072]{1,0:T(8,128)}) custom-call(bf16[4,256,768]{2,1,0:T(8,128)(2,1)S(1)} %bitcast.19, f32[256,3072]{1,0:T(8,128)S(1)} %copy-done.2, f32[256,3072]{1,0:T(8,128)S(1)} %copy-done.6, f32[256,3072]{1,0:T(8,128)S(1)} %copy-done.7), custom_call_target="tpu_custom_call" | custom-call | tf_op jit(solution)/shard_map/adam_matrix/pallas_call | solution.py:1150
  305.0 2.6 adam_matrix.5
  307.8 0.7 multiply_add_fusion.2
  308.6 0.6 multiply_add_fusion
  309.3 0.6 multiply_add_fusion.4
  309.9 0.6 fusion.7
  310.5 0.6 multiply_add_fusion.13
  311.1 0.6 fusion.8
  311.7 0.6 multiply_add_fusion.10
  312.3 0.6 copy.108
  312.9 1.0 copy.109
  313.9 1.0 copy.110
  (110 shorter events, 0.9 us)
Async XLA Ops:
  274.7 12.3 %copy-start.1 = (f32[1024,1024]{1,0:T(8,128)S(1)}, f32[1024,1024]{1,0:T(8,128)}, u32[]{:S(2)}) copy-start(f32[1024,1024]{1,0:T(8,128)} %refs_1_.9) | copy-start | bytes 12582916
  274.7 12.3 %copy-start.4 = (f32[1024,1024]{1,0:T(8,128)S(1)}, f32[1024,1024]{1,0:T(8,128)}, u32[]{:S(2)}) copy-start(f32[1024,1024]{1,0:T(8,128)} %refs_2_.9) | copy-start | bytes 12582916
  274.7 12.3 %copy-start.8 = (bf16[1024,1024]{1,0:T(8,128)(2,1)S(1)}, bf16[1024,1024]{1,0:T(8,128)(2,1)}, u32[]{:S(2)}) copy-start(bf16[1024,1024]{1,0:T(8,128)(2,1)} %get-tuple-element.110.refs_0_) | copy-start | bytes 6291460
  287.0 11.8 %copy-start.2 = (f32[256,3072]{1,0:T(8,128)S(1)}, f32[256,3072]{1,0:T(8,128)}, u32[]{:S(2)}) copy-start(f32[256,3072]{1,0:T(8,128)} %refs_1_.6) | copy-start | bytes 9437188
  287.0 11.8 %copy-start.6 = (f32[256,3072]{1,0:T(8,128)S(1)}, f32[256,3072]{1,0:T(8,128)}, u32[]{:S(2)}) copy-start(f32[256,3072]{1,0:T(8,128)} %refs_2_.6) | copy-start | bytes 9437188
  287.1 11.8 %copy-start.7 = (f32[256,3072]{1,0:T(8,128)S(1)}, f32[256,3072]{1,0:T(8,128)}, u32[]{:S(2)}) copy-start(f32[256,3072]{1,0:T(8,128)} %refs_3_.6) | copy-start | bytes 9437188
  287.1 11.8 %copy-start.10 = (bf16[1024,768]{1,0:T(8,128)(2,1)S(1)}, bf16[1024,768]{1,0:T(8,128)(2,1)}, u32[]{:S(2)}) copy-start(bf16[1024,768]{1,0:T(8,128)(2,1)} %get-tuple-element.104) | copy-start | bytes 4718596
  298.9 8.7 %copy-start.16 = (f32[16,1024]{1,0:T(8,128)S(1)}, f32[16,1024]{1,0:T(8,128)}, u32[]{:S(2)}) copy-start(f32[16,1024]{1,0:T(8,128)} %get-tuple-element.103) | copy-start | bytes 196612
  298.9 8.9 %copy-start.17 = (f32[768]{0:T(1024)S(1)}, f32[768]{0:T(1024)}, u32[]{:S(2)}) copy-start(f32[768]{0:T(1024)} %param.45) | copy-start | bytes 9220
  298.9 8.9 %copy-start.28 = (f32[768]{0:T(1024)S(1)}, f32[768]{0:T(1024)}, u32[]{:S(2)}) copy-start(f32[768]{0:T(1024)} %param.57) | copy-start | bytes 9220
  298.9 8.9 %copy-start.29 = (f32[768]{0:T(1024)S(1)}, f32[768]{0:T(1024)}, u32[]{:S(2)}) copy-start(f32[768]{0:T(1024)} %param.69) | copy-start | bytes 9220
  298.9 9.6 %copy-start.19 = (f32[1024]{0:T(1024)S(1)}, f32[1024]{0:T(1024)}, u32[]{:S(2)}) copy-start(f32[1024]{0:T(1024)} %param.49) | copy-start | bytes 12292
  298.9 9.6 %copy-start.30 = (f32[1024]{0:T(1024)S(1)}, f32[1024]{0:T(1024)}, u32[]{:S(2)}) copy-start(f32[1024]{0:T(1024)} %param.61) | copy-start | bytes 12292
  299.0 9.6 %copy-start.31 = (f32[1024]{0:T(1024)S(1)}, f32[1024]{0:T(1024)}, u32[]{:S(2)}) copy-start(f32[1024]{0:T(1024)} %param.73) | copy-start | bytes 12292
  299.0 10.3 %copy-start.26 = (f32[256]{0:T(256)S(1)}, f32[256]{0:T(256)}, u32[]{:S(2)}) copy-start(f32[256]{0:T(256)} %param.47) | copy-start | bytes 3076
  299.0 10.3 %copy-start.27 = (f32[256]{0:T(256)S(1)}, f32[256]{0:T(256)}, u32[]{:S(2)}) copy-start(f32[256]{0:T(256)} %param.51) | copy-start | bytes 3076
  299.0 10.3 %copy-start.40 = (f32[256]{0:T(256)S(1)}, f32[256]{0:T(256)}, u32[]{:S(2)}) copy-start(f32[256]{0:T(256)} %param.63) | copy-start | bytes 3076
  299.0 10.3 %copy-start.41 = (f32[256]{0:T(256)S(1)}, f32[256]{0:T(256)}, u32[]{:S(2)}) copy-start(f32[256]{0:T(256)} %param.75) | copy-start | bytes 3076
  299.0 10.3 %copy-start.42 = (f32[256]{0:T(256)S(1)}, f32[256]{0:T(256)}, u32[]{:S(2)}) copy-start(f32[256]{0:T(256)} %param.71) | copy-start | bytes 3076
  299.0 10.3 %copy-start.43 = (f32[256]{0:T(256)S(1)}, f32[256]{0:T(256)}, u32[]{:S(2)}) copy-start(f32[256]{0:T(256)} %param.59) | copy-start | bytes 3076
  299.0 10.8 %copy-start.36 = (f32[256]{0:T(256)S(1)}, f32[256]{0:T(256)}, u32[]{:S(2)}) copy-start(f32[256]{0:T(256)} %param.52) | copy-start | bytes 3076
  299.1 10.8 %copy-start.37 = (f32[256]{0:T(256)S(1)}, f32[256]{0:T(256)}, u32[]{:S(2)}) copy-start(f32[256]{0:T(256)} %param.64) | copy-start | bytes 3076
  299.1 11.4 %copy-start.20 = (f32[256]{0:T(256)S(1)}, f32[256]{0:T(256)}, u32[]{:S(2)}) copy-start(f32[256]{0:T(256)} %param.41) | copy-start | bytes 3076
  299.1 11.4 %copy-start.32 = (f32[256]{0:T(256)S(1)}, f32[256]{0:T(256)}, u32[]{:S(2)}) copy-start(f32[256]{0:T(256)} %param.53) | copy-start | bytes 3076
  299.1 11.4 %copy-start.33 = (f32[256]{0:T(256)S(1)}, f32[256]{0:T(256)}, u32[]{:S(2)}) copy-start(f32[256]{0:T(256)} %param.65) | copy-start | bytes 3076
  299.1 12.0 %copy-start.38 = (f32[256]{0:T(256)S(1)}, f32[256]{0:T(256)}, u32[]{:S(2)}) copy-start(f32[256]{0:T(256)} %param.54) | copy-start | bytes 3076
  299.1 12.0 %copy-start.39 = (f32[256]{0:T(256)S(1)}, f32[256]{0:T(256)}, u32[]{:S(2)}) copy-start(f32[256]{0:T(256)} %param.66) | copy-start | bytes 3076
  299.1 12.6 %copy-start.21 = (f32[256]{0:T(256)S(1)}, f32[256]{0:T(256)}, u32[]{:S(2)}) copy-start(f32[256]{0:T(256)} %param.43) | copy-start | bytes 3076
  299.1 12.6 %copy-start.34 = (f32[256]{0:T(256)S(1)}, f32[256]{0:T(256)}, u32[]{:S(2)}) copy-start(f32[256]{0:T(256)} %param.55) | copy-start | bytes 3076
  299.2 12.6 %copy-start.35 = (f32[256]{0:T(256)S(1)}, f32[256]{0:T(256)}, u32[]{:S(2)}) copy-start(f32[256]{0:T(256)} %param.67) | copy-start | bytes 3076
  305.0 7.9 %copy-start.15 = (bf16[512,1024]{1,0:T(8,128)(2,1)S(1)}, bf16[512,1024]{1,0:T(8,128)(2,1)}, u32[]{:S(2)}) copy-start(bf16[512,1024]{1,0:T(8,128)(2,1)} %get-tuple-element.314) | copy-start | bytes 3145732
  305.0 8.9 %copy-start.14 = (bf16[512,1024]{1,0:T(8,128)(2,1)S(1)}, bf16[512,1024]{1,0:T(8,128)(2,1)}, u32[]{:S(2)}) copy-start(bf16[512,1024]{1,0:T(8,128)(2,1)} %get-tuple-element.315) | copy-start | bytes 3145732
  (12 other events, 52.2 us)
where the time goes:
time: 316 us; the launch traced here: 315 us
  Pallas kernels  291 us (92%)
  local copies, waits for them, and re-layouts  17.8 us (6%)
  other arithmetic  5.12 us (2%)
    pallas_call x1, Pallas kernels, feed_phase(): pl.pallas_call(body, name='feed_phase', out_shape=outs, in_specs=[ANY] *...  164 us
    pallas_call x1, Pallas kernels, attention_phase(): pl.pallas_call(body, name='attention_phase', out_shape=outs, in_specs=[AN...  93.9 us
    pallas_call x4, Pallas kernels, adam_matrix(): pl.pallas_call(lambda *refs: adam_kernel(S, T, heads, *refs), name='adam_...  32.4 us
    unnamed x100, local copies, waits for them, and re-layouts  14.3 us

commit v1 on v0

--- a/solution.py
+++ b/solution.py
@@ -2,6 +2,7 @@
 
 import jax
 import jax.numpy as jnp
+import numpy as np
 from jax import lax
 from jax.experimental import pallas as pl
 from jax.experimental.pallas import tpu as pltpu
@@ -35,17 +36,14 @@
 
 
 def rotary_tables(length):
-    position = jnp.arange(length).astype(f32)[:, None]
+    position = np.arange(length, dtype=np.float32)[:, None]
     half = ROTARY // 2
-    inverse_freq = rope_base ** (-(jnp.arange(half).astype(f32) * 2.0 / ROTARY))
-    angles = position * inverse_freq[None, :]
-    return jnp.cos(angles), jnp.sin(angles)
-
-
-def rotate(tensor, cosine, sine):
-    half = ROTARY // 2
-    a, b, rest = tensor[..., :half], tensor[..., half:ROTARY], tensor[..., ROTARY:]
-    return jnp.concatenate([a * cosine - b * sine, b * cosine + a * sine, rest], -1)
+    inverse_freq = np.float32(rope_base) ** (-(np.arange(half, dtype=np.float32) * np.float32(2.0) / np.float32(ROTARY)))
+    angles = position * inverse_freq[None, :].astype(np.float32)
+    cosine, sine = np.cos(angles), np.sin(angles)
+    rest = np.zeros((length, HEAD_DIM - 2 * ROTARY), np.float32)
+    head = np.concatenate([cosine, cosine, -sine, sine, rest], 1)
+    return np.concatenate([head[: length // 2], head[length // 2 :]], 1).astype(np.float32)
 
 
 def dot32(a, b, dims):
@@ -228,13 +226,13 @@
 
 
 def attention_kernel(R, X, S, L, D, FT, *refs):
-    (x_ref, dy_ref, wt_m, wo_m, we_m, ws_m, sm_ref, rc_i, ra_i, rb_i) = refs[:10]
-    (xg, dyg, wt_o, wo_o, we_o, ws_o, vec_o, ctx_o, gt_o, wtl_o, wth_o, wol_o, woh_o, tbg_o) = refs[10:24]
+    (x_ref, dy_ref, wt_m, wo_m, we_m, ws_m, sm_ref, turn_i) = refs[:8]
+    (xg, dyg, wt_o, wo_o, we_o, ws_o, vec_o, ctx_o, gt_o, wtl_o, wth_o, wol_o, woh_o, tbg_o, n2_o) = refs[8:23]
     (
-        xs, dys, n1, gt, wtb, wob, smb, q_s, k_s, v_s, gc_s, kT, vT, ctxT, gqT, gk_a, gv_a, wtl, wth, wol, woh, wog,
-        rc_ref, ra_ref, rb_ref, wt_w, wo_w, we_w, ws_w, wt_ref, wo_ref, we_ref, ws_ref,
+        xs, dys, n1, n2, gt, wtb, wob, smb, q_s, k_s, v_s, gc_s, kT, vT, ctxT, gqT, gk_a, gv_a, wtl, wth, wol, woh, wog,
+        turn_s, turn_p, wt_w, wo_w, we_w, ws_w, wt_ref, wo_ref, we_ref, ws_ref,
         zs, zr, ys, yr, tok_s, tok_r, loc, cut,
-    ) = refs[24:]
+    ) = refs[23:]
     T = 2 * X
     rows = D // S
     DT = S * HEAD_DIM
@@ -317,7 +315,11 @@
     for c in own_copies:
         c.start()
 
-    tables = [local(a, b, cut.at[4 * S + 2 + q]) for q, (a, b) in enumerate(((rc_i, rc_ref), (ra_i, ra_ref), (rb_i, rb_ref)))]
+    tables = [local(turn_i, turn_p, cut.at[4 * S + 2])]
+
+    def table(q):
+        return jnp.concatenate([turn_s[q * L : (q + 1) * L, :]] * (DT // 128), 1)
+
     for c in tables:
         c.start()
     for c in cuts[2] + cuts[3]:
@@ -350,11 +352,14 @@
 
     def norm_one(i):
         gain, shift = vec_o[0:1, 0:D], vec_o[1:2, 0:D]
+        gain_b, shift_b = vec_o[2:3, 0:D], vec_o[3:4, 0:D]
 
         @pl.loop(0, L // 64)
         def _(b):
             at = rows_of(i * L + b * 64, 64)
-            n1[at, :] = (layer_norm_rows(xs[at, :]) * gain + shift).astype(bf16)
+            xhat = layer_norm_rows(xs[at, :])
+            n1[at, :] = (xhat * gain + shift).astype(bf16)
+            n2[at, :] = (xhat * gain_b + shift_b).astype(bf16)
 
     norm_one(0)
     g_wt.event(1)
@@ -369,14 +374,26 @@
     own_copies[4].wait()
     for c in tables:
         c.wait()
+    packed_turn = turn_p[...]
+    other_turn = pltpu.roll(packed_turn, HEAD_DIM, 1)
+    entry = lax.rem(lane, HEAD_DIM)
+    for b in range(2):
+        near, far = (packed_turn, other_turn) if b == 0 else (other_turn, packed_turn)
+        full = jnp.where(lane < HEAD_DIM, near, far)
+        moved = pltpu.roll(full, 128 - ROTARY, 1)
+        at = b * (L // 2)
+        turn_s[at : at + L // 2, :] = jnp.where(entry < ROTARY, full, 1.0)
+        turn_s[L + at : L + at + L // 2, :] = jnp.where(entry < ROTARY // 2, moved, 0.0)
+        upper = jnp.logical_and(entry >= ROTARY // 2, entry < ROTARY)
+        turn_s[2 * L + at : 2 * L + at + L // 2, :] = jnp.where(upper, moved, 0.0)
     g_wt.arrived()
     g_wo.arrived()
     late = [(g, step) for step in range(1, S) for g in (g_we, g_ws)]
 
     def pump(i, turn):
         for index in range(T):
-            at = 2 * (2 * index + turn)
-            todo = late[at : at + 2]
+            at = 2 * (2 * index + turn) - 2
+            todo = late[max(at, 0) : at + 2]
             if todo:
                 @pl.when(i == index)
                 def _():
@@ -395,9 +412,9 @@
             val = dot32(n1[here, :], wtb[:, j * DT : (j + 1) * DT], ONE) + vec_o[9 + j : 10 + j, 0:DT]
             if j < 2:
                 val = (
-                    val * rc_ref[...]
-                    + pltpu.roll(val, DT - 8, 1) * ra_ref[...]
-                    + pltpu.roll(val, 8, 1) * rb_ref[...]
+                    val * table(0)
+                    + pltpu.roll(val, DT - 8, 1) * table(1)
+                    + pltpu.roll(val, 8, 1) * table(2)
                 )
             vb = val.astype(bf16)
             if j == 0:
@@ -439,9 +456,9 @@
             else:
                 val = gqT[...].T if j == 0 else gk_a[...]
                 val = (
-                    val * rc_ref[...]
-                    - pltpu.roll(val, DT - 8, 1) * ra_ref[...]
-                    - pltpu.roll(val, 8, 1) * rb_ref[...]
+                    val * table(0)
+                    - pltpu.roll(val, DT - 8, 1) * table(1)
+                    - pltpu.roll(val, 8, 1) * table(2)
                 )
             gt[here, j * DT : (j + 1) * DT] = val.astype(bf16)
         ctx_o[:, rows_of(i * L, L)] = ctxT[...]
@@ -482,10 +499,11 @@
         local(wtb, wt_o, loc.at[3]),
         local(wob, wo_o, loc.at[4]),
         local(gt, gt_o, loc.at[7]),
+        local(n2, n2_o, loc.at[12]),
     ]
     for o in outs:
         o.start()
-    for g, step in late[4 * T :]:
+    for g, step in late[4 * T - 2 :]:
         g.event(step)
     ones = jnp.ones((8, T * L), bf16)
     tbg_o[...] = dot32(ones, gt[...], ONE)
@@ -548,34 +566,34 @@
         sds((n, D), bf16), sds((n, D), bf16), sds((D, 3 * DT), bf16), sds((DT, D), bf16),
         sds((D, FT), bf16), sds((FT, D), bf16), sds((16, max(D, FT)), f32), sds((DT, n), bf16),
         sds((n, 3 * DT), bf16), sds((D, 3 * DT), bf16), sds((D // R, 3 * DT), f32),
-        sds((DT, D), bf16), sds((DT // R, D), f32), sds((8, 3 * DT), f32),
+        sds((DT, D), bf16), sds((DT // R, D), f32), sds((8, 3 * DT), f32), sds((n, D), bf16),
     ]
-    specs = [ANY] * 6 + [VM, VM] + [ANY] * 5 + [VM]
+    specs = [ANY] * 6 + [VM, VM] + [ANY] * 5 + [VM, ANY]
     vmem = pltpu.VMEM
     scratch = [
-        vmem((n, D), bf16), vmem((n, D), bf16), vmem((n, D), bf16), vmem((n, 3 * DT), bf16),
+        vmem((n, D), bf16), vmem((n, D), bf16), vmem((n, D), bf16), vmem((n, D), bf16), vmem((n, 3 * DT), bf16),
         vmem((D, 3 * DT), bf16), vmem((DT, D), bf16), vmem((S * SMALL_ROWS, 128), f32),
         vmem((L, DT), bf16), vmem((L, DT), bf16), vmem((L, DT), bf16), vmem((L, DT), bf16),
         vmem((DT, L), bf16), vmem((DT, L), bf16), vmem((DT, L), bf16), vmem((DT, L), f32),
         vmem((L, DT), f32), vmem((L, DT), f32), vmem((D, 3 * DT), bf16), vmem((D // R, 3 * DT), f32),
         vmem((DT, D), bf16), vmem((DT // R, D), f32), vmem((DT, D), f32),
-        vmem((L, DT), f32), vmem((L, DT), f32), vmem((L, DT), f32),
+        vmem((3 * L, 128), f32), vmem((L // 2, 128), f32),
         vmem((rows, 3 * S * 128), f32), vmem((HEAD_DIM, D), f32), vmem((rows, FT), f32), vmem((fs, D), f32),
         vmem((rows, 3 * DT), bf16), vmem((HEAD_DIM, D), bf16), vmem((rows, FT), bf16), vmem((fs, D), bf16),
-        dma((5, S, 2)), dma((5, S)), dma((5, S, R)), dma((5, S, R)), dma((2, 4)), dma((2, 4)), dma((12,)), dma((4 * S + 5,)),
+        dma((5, S, 2)), dma((5, S)), dma((5, S, R)), dma((5, S, R)), dma((2, 4)), dma((2, 4)), dma((13,)), dma((4 * S + 5,)),
     ]
     body = lambda *refs: attention_kernel(R, X, S, L, D, FT, *refs)
     return pl.pallas_call(
         body,
         name="attention_phase",
         out_shape=outs,
-        in_specs=[ANY] * 10,
+        in_specs=[ANY] * 8,
         out_specs=specs,
         scratch_shapes=scratch,
         compiler_params=pltpu.CompilerParams(
             collective_id=1, has_side_effects=True, vmem_limit_bytes=60 * 1024 * 1024
         ),
-    )(x, dy, wt, wo, we, ws, small, *tables)
+    )(x, dy, wt, wo, we, ws, small, tables)
 
 
 class GradSum:
@@ -738,14 +756,14 @@
 
 
 def feed_kernel(R, X, S, L, D, FT, *refs):
-    (xg, dyg, wt_f, wo_f, we_f, ws_f, vec, ctx_i, gt_i, wtl, wth, wol, woh, tbg) = refs[:14]
-    (out_o, ing_o, g_wt, g_wo, g_we, g_ws, v_o) = refs[14:21]
-    rest = list(refs[21:])
+    (xg, dyg, wt_f, wo_f, we_f, ws_f, vec, ctx_i, gt_i, wtl, wth, wol, woh, tbg, n2_i) = refs[:15]
+    (out_o, ing_o, g_wt, g_wo, g_we, g_ws, v_o) = refs[15:22]
+    rest = list(refs[22:])
     take = lambda count: [rest.pop(0) for _ in range(count)]
     (xb, dyb, n2b, actb, ghb, web, wsb, wob, ctb) = take(9)
-    wt_bufs, wo_bufs, we_bufs, ws_bufs = take(5), take(5), take(6), take(6)
+    wt_bufs, wt2_bufs, wo_bufs, we_bufs, ws_bufs = take(5), take(5), take(5), take(6), take(6)
     (send_b, out_r, dx_r, xs_b, out_x, dx_x, vsum, vrecv) = take(8)
-    sem_sets = [dict(zip(SEM_NAMES, take(len(SEM_NAMES)))) for _ in range(4)]
+    sem_sets = [dict(zip(SEM_NAMES, take(len(SEM_NAMES)))) for _ in range(5)]
     (loc, tok, v_s, v_r, dxk) = take(5)
     T = 2 * X
     n = T * L
@@ -756,47 +774,44 @@
     k.barrier(every_plane=True)
     rank = lambda tx, core: tx * 2 + core
     mt, mo, me, ms = rows // R, HEAD_DIM // R, rows // R, fs // R
-    u_wt = GradSum(k, S, mt, [wtl] + wt_bufs, sem_sets[0],
-                   lambda f, tx, c, r: g_wt.at[rows_of(rank(tx, c) * rows + r * mt, mt)])
+    wide = 3 * DT // 2
+
+    def triple_half(c, bufs, sems):
+        cols = pl.ds(c * wide, wide)
+        return GradSum(k, S, mt, [wtl.at[:, cols]] + bufs, sems,
+                       lambda f, tx, core, r: g_wt.at[rows_of(rank(tx, core) * rows + r * mt, mt), cols])
+
+    u_wt, u_wt2 = triple_half(0, wt_bufs, sem_sets[0]), triple_half(1, wt2_bufs, sem_sets[4])
     u_wo = GradSum(k, S, mo, [wol] + wo_bufs, sem_sets[1],
                    lambda f, tx, c, r: g_wo.at[rows_of(rank(tx, c) * HEAD_DIM + r * mo, mo)])
     u_we = GradSum(k, S, me, we_bufs, sem_sets[2],
                    lambda f, tx, c, r: g_we.at[rows_of(r * me, me), rows_of((f * T + rank(tx, c)) * fs, fs)])
     u_ws = GradSum(k, 1, ms, ws_bufs, sem_sets[3],
                    lambda f, tx, c, r: g_ws.at[rows_of(rank(tx, c) * fs + r * ms, ms)], only=True)
-    first = (u_wt, u_wo)
+    first = (u_wo, u_wt, u_wt2)
     for u in first:
         u.send_across(0)
 
     def load_x(i, place):
         return local(xg.at[rows_of(i * L, L)], xb.at[pl.ds(place * L, L)], loc.at[place])
 
-    load_x(0, 0).start()
+    load_x(1, 0).start()
     loads = [
-        local(we_f, web, loc.at[2]), local(dyg, dyb, loc.at[3]), local(ws_f, wsb, loc.at[4]),
+        local(we_f, web, loc.at[2]), local(n2_i, n2b, loc.at[1 + 12]), local(dyg, dyb, loc.at[3]), local(ws_f, wsb, loc.at[4]),
         local(wo_f, wob, loc.at[5]), local(ctx_i, ctb, loc.at[6]),
-        local(wth, wt_bufs[0], loc.at[7]), local(woh, wo_bufs[0], loc.at[8]),
+        local(woh, wo_bufs[0], loc.at[8]),
+        local(wth.at[:, pl.ds(0, wide)], wt_bufs[0], loc.at[7]),
+        local(wth.at[:, pl.ds(wide, wide)], wt2_bufs[0], loc.at[14]),
     ]
     for c in loads:
         c.start()
 
-    gain1, gain2, shift2 = vec[0:1, 0:D], vec[2:3, 0:D], vec[3:4, 0:D]
-
-    def norm_two(i, place):
-        @pl.loop(0, L // 64)
-        def _(b):
-            n2b[rows_of(i * L + b * 64, 64), :] = (
-                layer_norm_rows(xb[pl.ds(pl.multiple_of(place * L + b * 64, 64), 64), :]) * gain2 + shift2
-            ).astype(bf16)
-
-    for i in range(T):
-        load_x(i, i % 2).wait()
-        if i + 1 < T:
-            load_x(i + 1, (i + 1) % 2).start()
-        norm_two(i, i % 2)
-    load_x(1, 0).start()
-    for c in loads[:3]:
+    gain1, gain2 = vec[0:1, 0:D], vec[2:3, 0:D]
+    for c in loads[:4]:
         c.wait()
+    for c in loads[6:9]:
+        c.wait()
+    early = {T * S // 4: u_wo, T * S // 2: u_wt, T * S - 1: u_wt2}
 
     def hidden_body(it, carry):
         i, f = it // S, lax.rem(it, S)
@@ -806,11 +821,15 @@
         actb[here, cols] = (h * cdf).astype(bf16)
         slope = cdf + h * (jnp.exp(-0.5 * h * h) * (1.0 / math.sqrt(2.0 * math.pi)))
         ghb[here, cols] = (dot32(dyb[here, :], wsb[cols, :], NT) * slope).astype(bf16)
+        for turn, u in early.items():
+            @pl.when(it == turn)
+            def _():
+                u.sum_across(0)
         return carry
 
     lax.fori_loop(0, T * S, hidden_body, 0)
-    loads[3].wait()
     loads[4].wait()
+    loads[5].wait()
     half = L // 2
 
     def feed_rows(i, b):
@@ -841,14 +860,7 @@
             xs_b[b * half : (b + 1) * half, :] = (feed_rows(2, b) + got).astype(bf16)
         to_tx(0).start()
 
-    for b in range(2):
-        dxk[b * half : (b + 1) * half, :] = feed_rows(0, b)
-
     side = D // DT
-    thirds = [wsb.at[pl.ds((j // side) * D, D), pl.ds((j % side) * DT, DT)] for j in range(3)]
-    load_wt = [local(wt_f.at[:, pl.ds(j * DT, DT)], thirds[j], loc.at[(9, 11, 12)[j]]) for j in range(3)]
-    for c in load_wt:
-        c.start()
 
     def triple_back(at):
         total = None
@@ -869,9 +881,6 @@
             def _():
                 u.keep[rows_of((f * u.B + block) * u.m, u.m), :] = part
 
-    loads[5].wait()
-    loads[6].wait()
-
     def chunk_body(f, carry):
         cols = pl.ds(pl.multiple_of(f * fs, fs), fs)
         store_grad(u_ws, f, 0, dot32(actb[:, cols], dyb[...], TN))
@@ -884,15 +893,17 @@
 
         lax.fori_loop(0, S, block_body, 0)
         u_we.send_across(f)
-
-        @pl.when(f == 0)
-        def _():
-            for u in first:
-                u.sum_across(0)
-
         return carry
 
     lax.fori_loop(0, S, chunk_body, 0)
+    for b in range(2):
+        dxk[b * half : (b + 1) * half, :] = feed_rows(0, b)
+
+    thirds = [wsb.at[pl.ds((j // side) * D, D), pl.ds((j % side) * DT, DT)] for j in range(3)]
+    load_wt = [local(wt_f.at[:, pl.ds(j * DT, DT)], thirds[j], loc.at[(9, 11, 12)[j]]) for j in range(3)]
+    for c in load_wt:
+        c.start()
+
     gtb = actb.at[:, pl.ds(0, 3 * DT)]
     load_gt = local(gt_i, gtb, loc.at[10])
     load_gt.start()
@@ -907,6 +918,9 @@
             getattr(u, step)(f)
 
     vsum[...] = jnp.zeros_like(vsum)
+    for u in first:
+        u.total(0)
+    pair("sum_across", 0)
 
     def slot_grad(i, place, finish):
         for b in range(2):
@@ -936,6 +950,14 @@
 
             slot_grad(i, place, finish)
             to_core(1, j).start()
+            if turn == 0:
+                for u in first:
+                    u.forward_rep(0)
+            else:
+                pair("sum_across", 1)
+                pair("total", 0)
+                for u in first:
+                    u.forward_tx(0)
         elif i == 2:
             to_core(1, 1).wait_recv()
 
@@ -945,9 +967,9 @@
 
             slot_grad(2, place, finish)
             to_tx(1).start()
-            pair("sum_across", 0)
-            for u in first:
-                u.total(0)
+            pair("sum_across", 2)
+            pair("total", 1)
+            pair("forward_rep", 0)
         else:
             to_core(0, 0).wait_recv()
             to_core(1, 0).wait_recv()
@@ -1001,9 +1023,6 @@
     ]
     exchange(at_stage, rep_copies)
     at_stage += R - 1
-    pair("sum_across", 1)
-    for u in first:
-        u.forward_rep(0)
     z_copies = [
         remote(
             vsum, vrecv.at[at_stage + dz - 1], v_s.at[at_stage + dz - 1], v_r.at[at_stage + dz - 1],
@@ -1013,16 +1032,19 @@
     ]
     for c in z_copies:
         c.start()
-    pair("total", 0)
-    for f in range(2, S):
+    if X == 1:
+        for u in first:
+            u.forward_tx(0)
+        pair("sum_across", 1)
+        pair("sum_across", 2)
+        pair("total", 0)
+        pair("total", 1)
+        pair("forward_rep", 0)
+    for f in range(3, S):
         pair("sum_across", f)
-        if f == 2:
-            for u in first:
-                u.forward_tx(0)
         pair("total", f - 1)
         pair("forward_rep", f - 2)
-        if f > 2:
-            pair("forward_tx", f - 3)
+        pair("forward_tx", f - 3)
     for c in z_copies:
         c.wait()
     total = vsum[...]
@@ -1061,7 +1083,7 @@
     save_ing.wait()
 
 
-def feed_phase(R, X, S, F, xg, dyg, wt_f, wo_f, we_f, ws_f, vecs, ctxT, gt, wtl, wth, wol, woh, tbg):
+def feed_phase(R, X, S, F, xg, dyg, wt_f, wo_f, we_f, ws_f, vecs, ctxT, gt, wtl, wth, wol, woh, tbg, n2):
     T = 2 * X
     n, D = xg.shape
     L = n // T
@@ -1091,27 +1113,27 @@
         vmem((D, FT), bf16), vmem((FT, D), bf16), vmem((DT, D), bf16),
         vmem((DT, n), bf16),
     ]
-    scratch += bufs(1, S, mt, 3 * DT, False, 1) + bufs(1, S, mo, D, False, 1)
+    scratch += bufs(1, S, mt, 3 * DT // 2, False, 1) * 2 + bufs(1, S, mo, D, False, 1)
     scratch += bufs(S, S, me, fs, True, S) + bufs(S, 1, ms, D, True, 1)
     scratch += [
         vmem((2 * L, D), bf16), vmem((X * L, D), bf16), vmem((X * L, D), bf16), vmem((2 * L, D), bf16),
         vmem((L, D), bf16), vmem((L, D), bf16), vmem((16, W), f32), vmem((2 + R - 1 + S - 1, 16, W), f32),
     ]
-    for count in (1, 1, S, S):
+    for count in (1, 1, S, S, 1):
         scratch += grad_sems(count, R, X, S)
-    scratch += [dma((13,)), dma((2, 3, 2)), dma((2 + R - 1 + S - 1,)), dma((2 + R - 1 + S - 1,)), vmem((L, D), f32)]
+    scratch += [dma((15,)), dma((2, 3, 2)), dma((2 + R - 1 + S - 1,)), dma((2 + R - 1 + S - 1,)), vmem((L, D), f32)]
     body = lambda *refs: feed_kernel(R, X, S, L, D, FT, *refs)
     return pl.pallas_call(
         body,
         name="feed_phase",
         out_shape=outs,
-        in_specs=[ANY] * 6 + [VM] + [ANY] * 6 + [VM],
+        in_specs=[ANY] * 6 + [VM] + [ANY] * 6 + [VM, ANY],
         out_specs=[ANY] * 6 + [VM],
         scratch_shapes=scratch,
         compiler_params=pltpu.CompilerParams(
             collective_id=2, has_side_effects=True, vmem_limit_bytes=67_000_000
         ),
-    )(xg, dyg, wt_f, wo_f, we_f, ws_f, vecs, ctxT, gt, wtl, wth, wol, woh, tbg)
+    )(xg, dyg, wt_f, wo_f, we_f, ws_f, vecs, ctxT, gt, wtl, wth, wol, woh, tbg, n2)
 
 
 def adam_kernel(S, T, heads, *refs):
@@ -1180,19 +1202,13 @@
 
         eb_own = lax.dynamic_slice_in_dim(masters[9], t * fs, fs, 0)
         packed = [masters[i] for i in (0, 1, 2, 3, 7, 11)] + [eb_own, masters[5]]
-        width = sum(v.shape[0] for v in packed)
-        packed.append(jnp.zeros((SMALL_ROWS * 128 - width,), f32))
-        small = lax.reduce_precision(jnp.concatenate(packed).reshape(SMALL_ROWS, 128), 8, 7)
-
-        cosine, sine = rotary_tables(L)
-        zero, one = jnp.zeros((L, 8), f32), jnp.ones((L, HEAD_DIM - 16), f32)
-        pad = jnp.zeros((L, HEAD_DIM - 16), f32)
-        tables = (
-            jnp.tile(jnp.concatenate([cosine, cosine, one], 1), (1, S)),
-            jnp.tile(jnp.concatenate([-sine, zero, pad], 1), (1, S)),
-            jnp.tile(jnp.concatenate([zero, sine, pad], 1), (1, S)),
-        )
-        passed = attention_phase(R, X, S, x, dy, wt, wo, we, ws, small, tables)
+        wide, at, flat = SMALL_ROWS * 128, 0, 0.0
+        for v in packed:
+            flat = flat + lax.pad(v, jnp.float32(0), [(at, wide - at - v.shape[0], 0)])
+            at += v.shape[0]
+        small = lax.reduce_precision(flat, 8, 7).reshape(SMALL_ROWS, 128)
+
+        passed = attention_phase(R, X, S, x, dy, wt, wo, we, ws, small, jnp.asarray(rotary_tables(L)))
         out, in_grad, wt_s, wo_s, we_s, ws_s, vec = feed_phase(R, X, S, F, *passed)
         wt_s = wt_s.reshape(T, rows, -1)
         DT, FT = S * HEAD_DIM, F // T

time: 316 us -> 316 us (level)
  local copies, waits for them, and re-layouts: 17.8 us -> 9.69 us
  Pallas kernels: 291 us -> 297 us
    pallas_call x1, Pallas kernels: 164 us -> 173 us  [feed_phase(): pl.pallas_call(body, name='feed_phase', out_shape=outs, in_specs=[ANY] *...]
    unnamed x100 -> x92, local copies, waits for them, and re-layouts: 14.3 us -> 8.71 us
where the time goes in v1:
time: 316 us; the launch traced here: 314 us
  Pallas kernels  297 us (94%)
  local copies, waits for them, and re-layouts  9.69 us (3%)
  other arithmetic  5.65 us (2%)
    pallas_call x1, Pallas kernels, feed_phase(): pl.pallas_call(body, name='feed_phase', out_shape=outs, in_specs=[ANY] *...  173 us
    pallas_call x1, Pallas kernels, attention_phase(): pl.pallas_call(body, name='attention_phase', out_shape=outs, in_specs=[AN...  91.1 us
    pallas_call x4, Pallas kernels, adam_matrix(): pl.pallas_call(lambda *refs: adam_kernel(S, T, heads, *refs), name='adam_...  32.4 us
    unnamed x92, local copies, waits for them, and re-layouts  8.71 us

profile of v1, /device:TPU:27, one launch (start us, length us, event | category | flops | bytes accessed | tf_op | source)
XLA Modules:
  0.0 313.6 jit_solution(1224966178919658778)
XLA Ops:
  0.7 0.8 dynamic_slice.34
  1.5 1.4 reduce-precision_bitcast_fusion.refs_6_
  2.9 91.1 %attention_phase.1 = (bf16[2048,1024]{1,0:T(8,128)(2,1)}, bf16[2048,1024]{1,0:T(8,128)(2,1)}, bf16[1024,768]{1,0:T(8,128)(2,1)}, bf16[256,1024]{1,0:T(8,128)(2,1...) custom-call(bf16[512,1024]{1,0:T(8,128)(2,1)} %refs_0_.1, ...), custom_call_target="tpu_custom_call" | custom-call | tf_op jit(solution)/shard_map/attention_phase/pallas_call | solution.py:586
  94.0 173.3 %feed_phase.1 = (bf16[512,1024]{1,0:T(8,128)(2,1)}, bf16[512,1024]{1,0:T(8,128)(2,1)}, bf16[1024,768]{1,0:T(8,128)(2,1)}, bf16[256,1024]{1,0:T(8,128)(2,1)}, bf1...) custom-call(bf16[2048,1024]{1,0:T(8,128)(2,1)} %get-tuple-element.88.refs_0_, ...), custom_call_target="tpu_custom_call" | custom-call | tf_op jit(solution)/shard_map/feed_phase/pallas_call | solution.py:1126
  267.3 2.2 copy-done
  269.5 2.2 copy-done.3
  271.7 1.6 copy-done.9
  273.3 12.3 %adam_matrix.6 = (f32[256,4096]{1,0:T(8,128)}, f32[256,4096]{1,0:T(8,128)}, f32[256,4096]{1,0:T(8,128)}, f32[256,4096]{1,0:T(8,128)}) custom-call(bf16[256,4096]{1,0:T(8,128)(2,1)S(1)} %copy-done.9, f32[256,4096]{1,0:T(8,128)S(1)} %copy-done, f32[256,4096]{1,0:T(8,128)S(1)} %copy-done.3, f32[256,4096]{1,0:T(8,128)} %refs_3_.8), custom_call_target="tpu_custom_call" | custom-call | tf_op jit(solution)/shard_map/adam_matrix/pallas_call | solution.py:1172
  285.6 0.0 copy-start.6
  285.6 0.0 copy-start.7
  285.6 11.7 %adam_matrix.7 = (f32[1024,1024]{1,0:T(8,128)}, f32[1024,1024]{1,0:T(8,128)}, f32[1024,1024]{1,0:T(8,128)}, f32[1024,1024]{1,0:T(8,128)}) custom-call(bf16[1024,1024]{1,0:T(8,128)(2,1)S(1)} %copy-done.8, f32[1024,1024]{1,0:T(8,128)S(1)} %copy-done.1, f32[1024,1024]{1,0:T(8,128)S(1)} %copy-done.4, f32[1024,1024]{1,0:T(8,128)} %refs_3_.9), custom_call_target="tpu_custom_call" | custom-call | tf_op jit(solution)/shard_map/adam_matrix/pallas_call | solution.py:1172
  297.4 0.0 copy-start.5
  297.4 0.0 copy-start.11
  297.5 0.0 copy-start.26
  297.5 0.0 copy-start.40
  297.5 0.0 copy-start.43
  297.7 5.8 %adam_matrix.4 = (f32[256,3072]{1,0:T(8,128)}, f32[256,3072]{1,0:T(8,128)}, f32[256,3072]{1,0:T(8,128)}, f32[256,3072]{1,0:T(8,128)}) custom-call(bf16[4,256,768]{2,1,0:T(8,128)(2,1)S(1)} %bitcast.16, f32[256,3072]{1,0:T(8,128)S(1)} %copy-done.2, f32[256,3072]{1,0:T(8,128)S(1)} %copy-done.6, f32[256,3072]{1,0:T(8,128)S(1)} %copy-done.7), custom_call_target="tpu_custom_call" | custom-call | tf_op jit(solution)/shard_map/adam_matrix/pallas_call | solution.py:1172
  303.6 2.6 adam_matrix.5
  306.2 0.0 copy-start.18
  306.2 0.0 copy-start.22
  306.3 0.6 multiply_add_fusion.4
  306.9 0.6 multiply_add_fusion.10
  307.5 0.6 multiply_add_fusion.13
  308.1 0.6 fusion.7
  308.7 0.1 reshape.125
  308.8 0.1 reshape.126
  308.9 0.7 multiply_add_fusion.2
  309.7 0.6 multiply_add_fusion
  310.3 0.6 fusion.6
  310.9 0.6 copy.97
  311.4 1.0 copy.98
  312.4 1.0 copy.99
  (84 shorter events, 0.3 us)
Async XLA Ops:
  273.3 12.3 %copy-start.1 = (f32[1024,1024]{1,0:T(8,128)S(1)}, f32[1024,1024]{1,0:T(8,128)}, u32[]{:S(2)}) copy-start(f32[1024,1024]{1,0:T(8,128)} %refs_1_.9) | copy-start | bytes 12582916
  273.3 12.3 %copy-start.4 = (f32[1024,1024]{1,0:T(8,128)S(1)}, f32[1024,1024]{1,0:T(8,128)}, u32[]{:S(2)}) copy-start(f32[1024,1024]{1,0:T(8,128)} %refs_2_.9) | copy-start | bytes 12582916
  273.3 12.3 %copy-start.8 = (bf16[1024,1024]{1,0:T(8,128)(2,1)S(1)}, bf16[1024,1024]{1,0:T(8,128)(2,1)}, u32[]{:S(2)}) copy-start(bf16[1024,1024]{1,0:T(8,128)(2,1)} %get-tuple-element.112.refs_0_) | copy-start | bytes 6291460
  285.6 11.8 %copy-start.2 = (f32[256,3072]{1,0:T(8,128)S(1)}, f32[256,3072]{1,0:T(8,128)}, u32[]{:S(2)}) copy-start(f32[256,3072]{1,0:T(8,128)} %refs_1_.6) | copy-start | bytes 9437188
  285.6 11.8 %copy-start.6 = (f32[256,3072]{1,0:T(8,128)S(1)}, f32[256,3072]{1,0:T(8,128)}, u32[]{:S(2)}) copy-start(f32[256,3072]{1,0:T(8,128)} %refs_2_.6) | copy-start | bytes 9437188
  285.6 11.8 %copy-start.7 = (f32[256,3072]{1,0:T(8,128)S(1)}, f32[256,3072]{1,0:T(8,128)}, u32[]{:S(2)}) copy-start(f32[256,3072]{1,0:T(8,128)} %refs_3_.6) | copy-start | bytes 9437188
  285.6 11.8 %copy-start.10 = (bf16[1024,768]{1,0:T(8,128)(2,1)S(1)}, bf16[1024,768]{1,0:T(8,128)(2,1)}, u32[]{:S(2)}) copy-start(bf16[1024,768]{1,0:T(8,128)(2,1)} %get-tuple-element.106) | copy-start | bytes 4718596
  297.4 8.7 %copy-start.16 = (f32[16,1024]{1,0:T(8,128)S(1)}, f32[16,1024]{1,0:T(8,128)}, u32[]{:S(2)}) copy-start(f32[16,1024]{1,0:T(8,128)} %get-tuple-element.105) | copy-start | bytes 196612
  297.5 8.8 %copy-start.25 = (f32[256]{0:T(256)S(1)}, f32[256]{0:T(256)}, u32[]{:S(2)}) copy-start(f32[256]{0:T(256)} %param.52) | copy-start | bytes 3076
  297.5 8.8 %copy-start.26 = (f32[256]{0:T(256)S(1)}, f32[256]{0:T(256)}, u32[]{:S(2)}) copy-start(f32[256]{0:T(256)} %param.48) | copy-start | bytes 3076
  297.5 8.8 %copy-start.40 = (f32[256]{0:T(256)S(1)}, f32[256]{0:T(256)}, u32[]{:S(2)}) copy-start(f32[256]{0:T(256)} %param.64) | copy-start | bytes 3076
  297.5 8.8 %copy-start.41 = (f32[256]{0:T(256)S(1)}, f32[256]{0:T(256)}, u32[]{:S(2)}) copy-start(f32[256]{0:T(256)} %param.76) | copy-start | bytes 3076
  297.5 8.8 %copy-start.42 = (f32[256]{0:T(256)S(1)}, f32[256]{0:T(256)}, u32[]{:S(2)}) copy-start(f32[256]{0:T(256)} %param.72) | copy-start | bytes 3076
  297.5 8.8 %copy-start.43 = (f32[256]{0:T(256)S(1)}, f32[256]{0:T(256)}, u32[]{:S(2)}) copy-start(f32[256]{0:T(256)} %param.60) | copy-start | bytes 3076
  297.5 9.4 %copy-start.20 = (f32[256]{0:T(256)S(1)}, f32[256]{0:T(256)}, u32[]{:S(2)}) copy-start(f32[256]{0:T(256)} %param.44) | copy-start | bytes 3076
  297.5 9.3 %copy-start.32 = (f32[256]{0:T(256)S(1)}, f32[256]{0:T(256)}, u32[]{:S(2)}) copy-start(f32[256]{0:T(256)} %param.56) | copy-start | bytes 3076
  297.6 9.3 %copy-start.33 = (f32[256]{0:T(256)S(1)}, f32[256]{0:T(256)}, u32[]{:S(2)}) copy-start(f32[256]{0:T(256)} %param.68) | copy-start | bytes 3076
  297.6 9.9 %copy-start.21 = (f32[256]{0:T(256)S(1)}, f32[256]{0:T(256)}, u32[]{:S(2)}) copy-start(f32[256]{0:T(256)} %param.42) | copy-start | bytes 3076
  297.6 9.9 %copy-start.34 = (f32[256]{0:T(256)S(1)}, f32[256]{0:T(256)}, u32[]{:S(2)}) copy-start(f32[256]{0:T(256)} %param.54) | copy-start | bytes 3076
  297.6 9.9 %copy-start.35 = (f32[256]{0:T(256)S(1)}, f32[256]{0:T(256)}, u32[]{:S(2)}) copy-start(f32[256]{0:T(256)} %param.66) | copy-start | bytes 3076
  297.6 10.5 %copy-start.36 = (f32[256]{0:T(256)S(1)}, f32[256]{0:T(256)}, u32[]{:S(2)}) copy-start(f32[256]{0:T(256)} %param.55) | copy-start | bytes 3076
  297.6 10.5 %copy-start.37 = (f32[256]{0:T(256)S(1)}, f32[256]{0:T(256)}, u32[]{:S(2)}) copy-start(f32[256]{0:T(256)} %param.67) | copy-start | bytes 3076
  297.6 11.3 %copy-start.17 = (f32[768]{0:T(1024)S(1)}, f32[768]{0:T(1024)}, u32[]{:S(2)}) copy-start(f32[768]{0:T(1024)} %param.46) | copy-start | bytes 9220
  297.6 11.3 %copy-start.28 = (f32[768]{0:T(1024)S(1)}, f32[768]{0:T(1024)}, u32[]{:S(2)}) copy-start(f32[768]{0:T(1024)} %param.58) | copy-start | bytes 9220
  297.7 11.2 %copy-start.29 = (f32[768]{0:T(1024)S(1)}, f32[768]{0:T(1024)}, u32[]{:S(2)}) copy-start(f32[768]{0:T(1024)} %param.70) | copy-start | bytes 9220
  297.7 12.0 %copy-start.19 = (f32[1024]{0:T(1024)S(1)}, f32[1024]{0:T(1024)}, u32[]{:S(2)}) copy-start(f32[1024]{0:T(1024)} %param.50) | copy-start | bytes 12292
  297.7 12.0 %copy-start.30 = (f32[1024]{0:T(1024)S(1)}, f32[1024]{0:T(1024)}, u32[]{:S(2)}) copy-start(f32[1024]{0:T(1024)} %param.62) | copy-start | bytes 12292
  297.7 12.0 %copy-start.31 = (f32[1024]{0:T(1024)S(1)}, f32[1024]{0:T(1024)}, u32[]{:S(2)}) copy-start(f32[1024]{0:T(1024)} %param.74) | copy-start | bytes 12292
  297.7 12.6 %copy-start.38 = (f32[256]{0:T(256)S(1)}, f32[256]{0:T(256)}, u32[]{:S(2)}) copy-start(f32[256]{0:T(256)} %param.53) | copy-start | bytes 3076
  297.7 12.6 %copy-start.39 = (f32[256]{0:T(256)S(1)}, f32[256]{0:T(256)}, u32[]{:S(2)}) copy-start(f32[256]{0:T(256)} %param.65) | copy-start | bytes 3076
  303.5 7.9 %copy-start.15 = (bf16[512,1024]{1,0:T(8,128)(2,1)S(1)}, bf16[512,1024]{1,0:T(8,128)(2,1)}, u32[]{:S(2)}) copy-start(bf16[512,1024]{1,0:T(8,128)(2,1)} %get-tuple-element.314) | copy-start | bytes 3145732
  303.5 8.9 %copy-start.14 = (bf16[512,1024]{1,0:T(8,128)(2,1)S(1)}, bf16[512,1024]{1,0:T(8,128)(2,1)}, u32[]{:S(2)}) copy-start(bf16[512,1024]{1,0:T(8,128)(2,1)} %get-tuple-element.315) | copy-start | bytes 3145732
  (12 other events, 59.8 us)

commit v2 on v1

--- a/solution.py
+++ b/solution.py
@@ -953,11 +953,6 @@
             if turn == 0:
                 for u in first:
                     u.forward_rep(0)
-            else:
-                pair("sum_across", 1)
-                pair("total", 0)
-                for u in first:
-                    u.forward_tx(0)
         elif i == 2:
             to_core(1, 1).wait_recv()
 
@@ -967,6 +962,10 @@
 
             slot_grad(2, place, finish)
             to_tx(1).start()
+            pair("sum_across", 1)
+            pair("total", 0)
+            for u in first:
+                u.forward_tx(0)
             pair("sum_across", 2)
             pair("total", 1)
             pair("forward_rep", 0)

time: 316 us -> 315 us (level)
  no operation moved by 1% of the time
where the time goes in v2:
time: 315 us; the launch traced here: 314 us
  Pallas kernels  297 us (94%)
  local copies, waits for them, and re-layouts  9.69 us (3%)
  other arithmetic  5.65 us (2%)
    pallas_call x1, Pallas kernels, feed_phase(): pl.pallas_call(body, name='feed_phase', out_shape=outs, in_specs=[ANY] *...  174 us
    pallas_call x1, Pallas kernels, attention_phase(): pl.pallas_call(body, name='attention_phase', out_shape=outs, in_specs=[AN...  91.1 us
    pallas_call x4, Pallas kernels, adam_matrix(): pl.pallas_call(lambda *refs: adam_kernel(S, T, heads, *refs), name='adam_...  32.4 us
    unnamed x92, local copies, waits for them, and re-layouts  8.71 us

profile of v2, /device:TPU:27, one launch (start us, length us, event | category | flops | bytes accessed | tf_op | source)
XLA Modules:
  0.0 314.1 jit_solution(16421778281185473505)
XLA Ops:
  0.7 0.8 dynamic_slice.34
  1.5 1.4 reduce-precision_bitcast_fusion.refs_6_
  2.9 91.1 %attention_phase.1 = (bf16[2048,1024]{1,0:T(8,128)(2,1)}, bf16[2048,1024]{1,0:T(8,128)(2,1)}, bf16[1024,768]{1,0:T(8,128)(2,1)}, bf16[256,1024]{1,0:T(8,128)(2,1...) custom-call(bf16[512,1024]{1,0:T(8,128)(2,1)} %refs_0_.1, ...), custom_call_target="tpu_custom_call" | custom-call | tf_op jit(solution)/shard_map/attention_phase/pallas_call | solution.py:586
  94.0 173.8 %feed_phase.1 = (bf16[512,1024]{1,0:T(8,128)(2,1)}, bf16[512,1024]{1,0:T(8,128)(2,1)}, bf16[1024,768]{1,0:T(8,128)(2,1)}, bf16[256,1024]{1,0:T(8,128)(2,1)}, bf1...) custom-call(bf16[2048,1024]{1,0:T(8,128)(2,1)} %get-tuple-element.88.refs_0_, ...), custom_call_target="tpu_custom_call" | custom-call | tf_op jit(solution)/shard_map/feed_phase/pallas_call | solution.py:1125
  267.8 0.0 copy-start
  267.8 2.2 copy-done
  270.0 2.2 copy-done.3
  272.1 1.6 copy-done.9
  273.7 12.3 %adam_matrix.6 = (f32[256,4096]{1,0:T(8,128)}, f32[256,4096]{1,0:T(8,128)}, f32[256,4096]{1,0:T(8,128)}, f32[256,4096]{1,0:T(8,128)}) custom-call(bf16[256,4096]{1,0:T(8,128)(2,1)S(1)} %copy-done.9, f32[256,4096]{1,0:T(8,128)S(1)} %copy-done, f32[256,4096]{1,0:T(8,128)S(1)} %copy-done.3, f32[256,4096]{1,0:T(8,128)} %refs_3_.8), custom_call_target="tpu_custom_call" | custom-call | tf_op jit(solution)/shard_map/adam_matrix/pallas_call | solution.py:1171
  286.0 0.0 copy-start.2
  286.1 11.7 %adam_matrix.7 = (f32[1024,1024]{1,0:T(8,128)}, f32[1024,1024]{1,0:T(8,128)}, f32[1024,1024]{1,0:T(8,128)}, f32[1024,1024]{1,0:T(8,128)}) custom-call(bf16[1024,1024]{1,0:T(8,128)(2,1)S(1)} %copy-done.8, f32[1024,1024]{1,0:T(8,128)S(1)} %copy-done.1, f32[1024,1024]{1,0:T(8,128)S(1)} %copy-done.4, f32[1024,1024]{1,0:T(8,128)} %refs_3_.9), custom_call_target="tpu_custom_call" | custom-call | tf_op jit(solution)/shard_map/adam_matrix/pallas_call | solution.py:1171
  297.9 0.0 copy-start.12
  297.9 0.0 copy-start.25
  297.9 0.0 copy-start.41
  298.0 0.0 copy-start.42
  298.0 0.0 copy-start.20
  298.2 5.8 %adam_matrix.4 = (f32[256,3072]{1,0:T(8,128)}, f32[256,3072]{1,0:T(8,128)}, f32[256,3072]{1,0:T(8,128)}, f32[256,3072]{1,0:T(8,128)}) custom-call(bf16[4,256,768]{2,1,0:T(8,128)(2,1)S(1)} %bitcast.16, f32[256,3072]{1,0:T(8,128)S(1)} %copy-done.2, f32[256,3072]{1,0:T(8,128)S(1)} %copy-done.6, f32[256,3072]{1,0:T(8,128)S(1)} %copy-done.7), custom_call_target="tpu_custom_call" | custom-call | tf_op jit(solution)/shard_map/adam_matrix/pallas_call | solution.py:1171
  304.0 2.6 adam_matrix.5
  306.7 0.0 copy-start.18
  306.7 0.0 copy-start.22
  306.7 0.6 multiply_add_fusion.4
  307.4 0.6 multiply_add_fusion.10
  308.0 0.6 multiply_add_fusion.13
  308.6 0.6 fusion.7
  309.2 0.1 reshape.125
  309.3 0.1 reshape.126
  309.4 0.7 multiply_add_fusion.2
  310.1 0.6 multiply_add_fusion
  310.7 0.6 fusion.6
  311.3 0.6 copy.97
  311.9 1.0 copy.98
  312.9 1.0 copy.99
  (84 shorter events, 0.3 us)
Async XLA Ops:
  273.7 12.3 %copy-start.1 = (f32[1024,1024]{1,0:T(8,128)S(1)}, f32[1024,1024]{1,0:T(8,128)}, u32[]{:S(2)}) copy-start(f32[1024,1024]{1,0:T(8,128)} %refs_1_.9) | copy-start | bytes 12582916
  273.7 12.3 %copy-start.4 = (f32[1024,1024]{1,0:T(8,128)S(1)}, f32[1024,1024]{1,0:T(8,128)}, u32[]{:S(2)}) copy-start(f32[1024,1024]{1,0:T(8,128)} %refs_2_.9) | copy-start | bytes 12582916
  273.7 12.3 %copy-start.8 = (bf16[1024,1024]{1,0:T(8,128)(2,1)S(1)}, bf16[1024,1024]{1,0:T(8,128)(2,1)}, u32[]{:S(2)}) copy-start(bf16[1024,1024]{1,0:T(8,128)(2,1)} %get-tuple-element.112.refs_0_) | copy-start | bytes 6291460
  286.0 11.8 %copy-start.2 = (f32[256,3072]{1,0:T(8,128)S(1)}, f32[256,3072]{1,0:T(8,128)}, u32[]{:S(2)}) copy-start(f32[256,3072]{1,0:T(8,128)} %refs_1_.6) | copy-start | bytes 9437188
  286.1 11.8 %copy-start.6 = (f32[256,3072]{1,0:T(8,128)S(1)}, f32[256,3072]{1,0:T(8,128)}, u32[]{:S(2)}) copy-start(f32[256,3072]{1,0:T(8,128)} %refs_2_.6) | copy-start | bytes 9437188
  286.1 11.8 %copy-start.7 = (f32[256,3072]{1,0:T(8,128)S(1)}, f32[256,3072]{1,0:T(8,128)}, u32[]{:S(2)}) copy-start(f32[256,3072]{1,0:T(8,128)} %refs_3_.6) | copy-start | bytes 9437188
  286.1 11.8 %copy-start.10 = (bf16[1024,768]{1,0:T(8,128)(2,1)S(1)}, bf16[1024,768]{1,0:T(8,128)(2,1)}, u32[]{:S(2)}) copy-start(bf16[1024,768]{1,0:T(8,128)(2,1)} %get-tuple-element.106) | copy-start | bytes 4718596
  297.9 8.7 %copy-start.16 = (f32[16,1024]{1,0:T(8,128)S(1)}, f32[16,1024]{1,0:T(8,128)}, u32[]{:S(2)}) copy-start(f32[16,1024]{1,0:T(8,128)} %get-tuple-element.105) | copy-start | bytes 196612
  297.9 8.8 %copy-start.25 = (f32[256]{0:T(256)S(1)}, f32[256]{0:T(256)}, u32[]{:S(2)}) copy-start(f32[256]{0:T(256)} %param.52) | copy-start | bytes 3076
  297.9 8.8 %copy-start.26 = (f32[256]{0:T(256)S(1)}, f32[256]{0:T(256)}, u32[]{:S(2)}) copy-start(f32[256]{0:T(256)} %param.48) | copy-start | bytes 3076
  297.9 8.8 %copy-start.40 = (f32[256]{0:T(256)S(1)}, f32[256]{0:T(256)}, u32[]{:S(2)}) copy-start(f32[256]{0:T(256)} %param.64) | copy-start | bytes 3076
  297.9 8.8 %copy-start.41 = (f32[256]{0:T(256)S(1)}, f32[256]{0:T(256)}, u32[]{:S(2)}) copy-start(f32[256]{0:T(256)} %param.76) | copy-start | bytes 3076
  298.0 8.8 %copy-start.42 = (f32[256]{0:T(256)S(1)}, f32[256]{0:T(256)}, u32[]{:S(2)}) copy-start(f32[256]{0:T(256)} %param.72) | copy-start | bytes 3076
  298.0 8.8 %copy-start.43 = (f32[256]{0:T(256)S(1)}, f32[256]{0:T(256)}, u32[]{:S(2)}) copy-start(f32[256]{0:T(256)} %param.60) | copy-start | bytes 3076
  298.0 9.4 %copy-start.20 = (f32[256]{0:T(256)S(1)}, f32[256]{0:T(256)}, u32[]{:S(2)}) copy-start(f32[256]{0:T(256)} %param.44) | copy-start | bytes 3076
  298.0 9.3 %copy-start.32 = (f32[256]{0:T(256)S(1)}, f32[256]{0:T(256)}, u32[]{:S(2)}) copy-start(f32[256]{0:T(256)} %param.56) | copy-start | bytes 3076
  298.0 9.3 %copy-start.33 = (f32[256]{0:T(256)S(1)}, f32[256]{0:T(256)}, u32[]{:S(2)}) copy-start(f32[256]{0:T(256)} %param.68) | copy-start | bytes 3076
  298.0 9.9 %copy-start.21 = (f32[256]{0:T(256)S(1)}, f32[256]{0:T(256)}, u32[]{:S(2)}) copy-start(f32[256]{0:T(256)} %param.42) | copy-start | bytes 3076
  298.0 9.9 %copy-start.34 = (f32[256]{0:T(256)S(1)}, f32[256]{0:T(256)}, u32[]{:S(2)}) copy-start(f32[256]{0:T(256)} %param.54) | copy-start | bytes 3076
  298.0 9.9 %copy-start.35 = (f32[256]{0:T(256)S(1)}, f32[256]{0:T(256)}, u32[]{:S(2)}) copy-start(f32[256]{0:T(256)} %param.66) | copy-start | bytes 3076
  298.1 10.5 %copy-start.36 = (f32[256]{0:T(256)S(1)}, f32[256]{0:T(256)}, u32[]{:S(2)}) copy-start(f32[256]{0:T(256)} %param.55) | copy-start | bytes 3076
  298.1 10.5 %copy-start.37 = (f32[256]{0:T(256)S(1)}, f32[256]{0:T(256)}, u32[]{:S(2)}) copy-start(f32[256]{0:T(256)} %param.67) | copy-start | bytes 3076
  298.1 11.3 %copy-start.17 = (f32[768]{0:T(1024)S(1)}, f32[768]{0:T(1024)}, u32[]{:S(2)}) copy-start(f32[768]{0:T(1024)} %param.46) | copy-start | bytes 9220
  298.1 11.3 %copy-start.28 = (f32[768]{0:T(1024)S(1)}, f32[768]{0:T(1024)}, u32[]{:S(2)}) copy-start(f32[768]{0:T(1024)} %param.58) | copy-start | bytes 9220
  298.1 11.2 %copy-start.29 = (f32[768]{0:T(1024)S(1)}, f32[768]{0:T(1024)}, u32[]{:S(2)}) copy-start(f32[768]{0:T(1024)} %param.70) | copy-start | bytes 9220
  298.1 12.0 %copy-start.19 = (f32[1024]{0:T(1024)S(1)}, f32[1024]{0:T(1024)}, u32[]{:S(2)}) copy-start(f32[1024]{0:T(1024)} %param.50) | copy-start | bytes 12292
  298.1 12.0 %copy-start.30 = (f32[1024]{0:T(1024)S(1)}, f32[1024]{0:T(1024)}, u32[]{:S(2)}) copy-start(f32[1024]{0:T(1024)} %param.62) | copy-start | bytes 12292
  298.1 12.0 %copy-start.31 = (f32[1024]{0:T(1024)S(1)}, f32[1024]{0:T(1024)}, u32[]{:S(2)}) copy-start(f32[1024]{0:T(1024)} %param.74) | copy-start | bytes 12292
  298.2 12.6 %copy-start.38 = (f32[256]{0:T(256)S(1)}, f32[256]{0:T(256)}, u32[]{:S(2)}) copy-start(f32[256]{0:T(256)} %param.53) | copy-start | bytes 3076
  298.2 12.6 %copy-start.39 = (f32[256]{0:T(256)S(1)}, f32[256]{0:T(256)}, u32[]{:S(2)}) copy-start(f32[256]{0:T(256)} %param.65) | copy-start | bytes 3076
  304.0 7.9 %copy-start.15 = (bf16[512,1024]{1,0:T(8,128)(2,1)S(1)}, bf16[512,1024]{1,0:T(8,128)(2,1)}, u32[]{:S(2)}) copy-start(bf16[512,1024]{1,0:T(8,128)(2,1)} %get-tuple-element.314) | copy-start | bytes 3145732
  304.0 8.9 %copy-start.14 = (bf16[512,1024]{1,0:T(8,128)(2,1)S(1)}, bf16[512,1024]{1,0:T(8,128)(2,1)}, u32[]{:S(2)}) copy-start(bf16[512,1024]{1,0:T(8,128)(2,1)} %get-tuple-element.315) | copy-start | bytes 3145732
  (12 other events, 59.8 us)

commit v3 on v2

--- a/solution.py
+++ b/solution.py
@@ -885,6 +885,10 @@
         cols = pl.ds(pl.multiple_of(f * fs, fs), fs)
         store_grad(u_ws, f, 0, dot32(actb[:, cols], dyb[...], TN))
         u_ws.send_across(f)
+        return carry
+
+    def expand_body(f, carry):
+        cols = pl.ds(pl.multiple_of(f * fs, fs), fs)
 
         def block_body(p, c2):
             grad = dot32(n2b[:, pl.ds(pl.multiple_of(p * rows, rows), rows)], ghb[:, cols], TN)
@@ -896,6 +900,7 @@
         return carry
 
     lax.fori_loop(0, S, chunk_body, 0)
+    lax.fori_loop(0, S, expand_body, 0)
     for b in range(2):
         dxk[b * half : (b + 1) * half, :] = feed_rows(0, b)
 
@@ -913,8 +918,10 @@
     for c in load_wt:
         c.wait()
 
-    def pair(step, f):
-        for u in (u_we, u_ws):
+    queue = [(u_ws, f) for f in range(S)] + [(u_we, f) for f in range(S)]
+
+    def pair(step, stage):
+        for u, f in queue[2 * stage : 2 * stage + 2]:
             getattr(u, step)(f)
 
     vsum[...] = jnp.zeros_like(vsum)

time: 315 us -> 307 us (0.975); the launches traced: 314 us -> 303 us
  Pallas kernels: 297 us -> 286 us
    pallas_call x1, Pallas kernels: 174 us -> 162 us  [feed_phase(): pl.pallas_call(body, name='feed_phase', out_shape=outs, in_specs=[ANY] *...]
where the time goes in v3:
time: 307 us; the launch traced here: 303 us
  Pallas kernels  286 us (93%)
  local copies, waits for them, and re-layouts  9.69 us (3%)
  other arithmetic  5.65 us (2%)
    pallas_call x1, Pallas kernels, feed_phase(): pl.pallas_call(body, name='feed_phase', out_shape=outs, in_specs=[ANY] *...  162 us
    pallas_call x1, Pallas kernels, attention_phase(): pl.pallas_call(body, name='attention_phase', out_shape=outs, in_specs=[AN...  91.1 us
    pallas_call x4, Pallas kernels, adam_matrix(): pl.pallas_call(lambda *refs: adam_kernel(S, T, heads, *refs), name='adam_...  32.4 us
    unnamed x92, local copies, waits for them, and re-layouts  8.71 us

profile of v3, /device:TPU:27, one launch (start us, length us, event | category | flops | bytes accessed | tf_op | source)
XLA Modules:
  0.0 302.6 jit_solution(5727645968387035444)
XLA Ops:
  0.7 0.8 dynamic_slice.34
  1.5 1.4 reduce-precision_bitcast_fusion.refs_6_
  2.9 91.1 %attention_phase.1 = (bf16[2048,1024]{1,0:T(8,128)(2,1)}, bf16[2048,1024]{1,0:T(8,128)(2,1)}, bf16[1024,768]{1,0:T(8,128)(2,1)}, bf16[256,1024]{1,0:T(8,128)(2,1...) custom-call(bf16[512,1024]{1,0:T(8,128)(2,1)} %refs_0_.1, ...), custom_call_target="tpu_custom_call" | custom-call | tf_op jit(solution)/shard_map/attention_phase/pallas_call | solution.py:586
  94.0 162.3 %feed_phase.1 = (bf16[512,1024]{1,0:T(8,128)(2,1)}, bf16[512,1024]{1,0:T(8,128)(2,1)}, bf16[1024,768]{1,0:T(8,128)(2,1)}, bf16[256,1024]{1,0:T(8,128)(2,1)}, bf1...) custom-call(bf16[2048,1024]{1,0:T(8,128)(2,1)} %get-tuple-element.88.refs_0_, ...), custom_call_target="tpu_custom_call" | custom-call | tf_op jit(solution)/shard_map/feed_phase/pallas_call | solution.py:1132
  256.3 0.0 copy-start
  256.3 2.2 copy-done
  258.5 2.2 copy-done.3
  260.7 1.6 copy-done.9
  262.3 12.3 %adam_matrix.6 = (f32[256,4096]{1,0:T(8,128)}, f32[256,4096]{1,0:T(8,128)}, f32[256,4096]{1,0:T(8,128)}, f32[256,4096]{1,0:T(8,128)}) custom-call(bf16[256,4096]{1,0:T(8,128)(2,1)S(1)} %copy-done.9, f32[256,4096]{1,0:T(8,128)S(1)} %copy-done, f32[256,4096]{1,0:T(8,128)S(1)} %copy-done.3, f32[256,4096]{1,0:T(8,128)} %refs_3_.8), custom_call_target="tpu_custom_call" | custom-call | tf_op jit(solution)/shard_map/adam_matrix/pallas_call | solution.py:1178
  274.6 0.0 copy-start.2
  274.6 0.0 copy-start.6
  274.6 11.7 %adam_matrix.7 = (f32[1024,1024]{1,0:T(8,128)}, f32[1024,1024]{1,0:T(8,128)}, f32[1024,1024]{1,0:T(8,128)}, f32[1024,1024]{1,0:T(8,128)}) custom-call(bf16[1024,1024]{1,0:T(8,128)(2,1)S(1)} %copy-done.8, f32[1024,1024]{1,0:T(8,128)S(1)} %copy-done.1, f32[1024,1024]{1,0:T(8,128)S(1)} %copy-done.4, f32[1024,1024]{1,0:T(8,128)} %refs_3_.9), custom_call_target="tpu_custom_call" | custom-call | tf_op jit(solution)/shard_map/adam_matrix/pallas_call | solution.py:1178
  286.4 0.0 copy-start.5
  286.4 0.0 copy-start.25
  286.4 0.0 copy-start.26
  286.5 0.0 copy-start.42
  286.7 5.8 %adam_matrix.4 = (f32[256,3072]{1,0:T(8,128)}, f32[256,3072]{1,0:T(8,128)}, f32[256,3072]{1,0:T(8,128)}, f32[256,3072]{1,0:T(8,128)}) custom-call(bf16[4,256,768]{2,1,0:T(8,128)(2,1)S(1)} %bitcast.16, f32[256,3072]{1,0:T(8,128)S(1)} %copy-done.2, f32[256,3072]{1,0:T(8,128)S(1)} %copy-done.6, f32[256,3072]{1,0:T(8,128)S(1)} %copy-done.7), custom_call_target="tpu_custom_call" | custom-call | tf_op jit(solution)/shard_map/adam_matrix/pallas_call | solution.py:1178
  292.5 2.6 adam_matrix.5
  295.2 0.0 copy-start.18
  295.2 0.0 copy-start.22
  295.3 0.6 multiply_add_fusion.4
  295.9 0.6 multiply_add_fusion.10
  296.5 0.6 multiply_add_fusion.13
  297.1 0.6 fusion.7
  297.7 0.1 reshape.125
  297.8 0.1 reshape.126
  297.9 0.7 multiply_add_fusion.2
  298.6 0.6 multiply_add_fusion
  299.3 0.6 fusion.6
  299.8 0.6 copy.97
  300.4 1.0 copy.98
  301.4 1.0 copy.99
  (84 shorter events, 0.3 us)
Async XLA Ops:
  262.3 12.3 %copy-start.1 = (f32[1024,1024]{1,0:T(8,128)S(1)}, f32[1024,1024]{1,0:T(8,128)}, u32[]{:S(2)}) copy-start(f32[1024,1024]{1,0:T(8,128)} %refs_1_.9) | copy-start | bytes 12582916
  262.3 12.3 %copy-start.4 = (f32[1024,1024]{1,0:T(8,128)S(1)}, f32[1024,1024]{1,0:T(8,128)}, u32[]{:S(2)}) copy-start(f32[1024,1024]{1,0:T(8,128)} %refs_2_.9) | copy-start | bytes 12582916
  262.3 12.3 %copy-start.8 = (bf16[1024,1024]{1,0:T(8,128)(2,1)S(1)}, bf16[1024,1024]{1,0:T(8,128)(2,1)}, u32[]{:S(2)}) copy-start(bf16[1024,1024]{1,0:T(8,128)(2,1)} %get-tuple-element.112.refs_0_) | copy-start | bytes 6291460
  274.6 11.8 %copy-start.2 = (f32[256,3072]{1,0:T(8,128)S(1)}, f32[256,3072]{1,0:T(8,128)}, u32[]{:S(2)}) copy-start(f32[256,3072]{1,0:T(8,128)} %refs_1_.6) | copy-start | bytes 9437188
  274.6 11.8 %copy-start.6 = (f32[256,3072]{1,0:T(8,128)S(1)}, f32[256,3072]{1,0:T(8,128)}, u32[]{:S(2)}) copy-start(f32[256,3072]{1,0:T(8,128)} %refs_2_.6) | copy-start | bytes 9437188
  274.6 11.8 %copy-start.7 = (f32[256,3072]{1,0:T(8,128)S(1)}, f32[256,3072]{1,0:T(8,128)}, u32[]{:S(2)}) copy-start(f32[256,3072]{1,0:T(8,128)} %refs_3_.6) | copy-start | bytes 9437188
  274.6 11.8 %copy-start.10 = (bf16[1024,768]{1,0:T(8,128)(2,1)S(1)}, bf16[1024,768]{1,0:T(8,128)(2,1)}, u32[]{:S(2)}) copy-start(bf16[1024,768]{1,0:T(8,128)(2,1)} %get-tuple-element.106) | copy-start | bytes 4718596
  286.4 8.7 %copy-start.16 = (f32[16,1024]{1,0:T(8,128)S(1)}, f32[16,1024]{1,0:T(8,128)}, u32[]{:S(2)}) copy-start(f32[16,1024]{1,0:T(8,128)} %get-tuple-element.105) | copy-start | bytes 196612
  286.4 8.8 %copy-start.25 = (f32[256]{0:T(256)S(1)}, f32[256]{0:T(256)}, u32[]{:S(2)}) copy-start(f32[256]{0:T(256)} %param.52) | copy-start | bytes 3076
  286.4 8.8 %copy-start.26 = (f32[256]{0:T(256)S(1)}, f32[256]{0:T(256)}, u32[]{:S(2)}) copy-start(f32[256]{0:T(256)} %param.48) | copy-start | bytes 3076
  286.5 8.8 %copy-start.40 = (f32[256]{0:T(256)S(1)}, f32[256]{0:T(256)}, u32[]{:S(2)}) copy-start(f32[256]{0:T(256)} %param.64) | copy-start | bytes 3076
  286.5 8.8 %copy-start.41 = (f32[256]{0:T(256)S(1)}, f32[256]{0:T(256)}, u32[]{:S(2)}) copy-start(f32[256]{0:T(256)} %param.76) | copy-start | bytes 3076
  286.5 8.8 %copy-start.42 = (f32[256]{0:T(256)S(1)}, f32[256]{0:T(256)}, u32[]{:S(2)}) copy-start(f32[256]{0:T(256)} %param.72) | copy-start | bytes 3076
  286.5 8.8 %copy-start.43 = (f32[256]{0:T(256)S(1)}, f32[256]{0:T(256)}, u32[]{:S(2)}) copy-start(f32[256]{0:T(256)} %param.60) | copy-start | bytes 3076
  286.5 9.4 %copy-start.20 = (f32[256]{0:T(256)S(1)}, f32[256]{0:T(256)}, u32[]{:S(2)}) copy-start(f32[256]{0:T(256)} %param.44) | copy-start | bytes 3076
  286.5 9.3 %copy-start.32 = (f32[256]{0:T(256)S(1)}, f32[256]{0:T(256)}, u32[]{:S(2)}) copy-start(f32[256]{0:T(256)} %param.56) | copy-start | bytes 3076
  286.5 9.3 %copy-start.33 = (f32[256]{0:T(256)S(1)}, f32[256]{0:T(256)}, u32[]{:S(2)}) copy-start(f32[256]{0:T(256)} %param.68) | copy-start | bytes 3076
  286.5 9.9 %copy-start.21 = (f32[256]{0:T(256)S(1)}, f32[256]{0:T(256)}, u32[]{:S(2)}) copy-start(f32[256]{0:T(256)} %param.42) | copy-start | bytes 3076
  286.5 9.9 %copy-start.34 = (f32[256]{0:T(256)S(1)}, f32[256]{0:T(256)}, u32[]{:S(2)}) copy-start(f32[256]{0:T(256)} %param.54) | copy-start | bytes 3076
  286.6 9.9 %copy-start.35 = (f32[256]{0:T(256)S(1)}, f32[256]{0:T(256)}, u32[]{:S(2)}) copy-start(f32[256]{0:T(256)} %param.66) | copy-start | bytes 3076
  286.6 10.5 %copy-start.36 = (f32[256]{0:T(256)S(1)}, f32[256]{0:T(256)}, u32[]{:S(2)}) copy-start(f32[256]{0:T(256)} %param.55) | copy-start | bytes 3076
  286.6 10.5 %copy-start.37 = (f32[256]{0:T(256)S(1)}, f32[256]{0:T(256)}, u32[]{:S(2)}) copy-start(f32[256]{0:T(256)} %param.67) | copy-start | bytes 3076
  286.6 11.3 %copy-start.17 = (f32[768]{0:T(1024)S(1)}, f32[768]{0:T(1024)}, u32[]{:S(2)}) copy-start(f32[768]{0:T(1024)} %param.46) | copy-start | bytes 9220
  286.6 11.3 %copy-start.28 = (f32[768]{0:T(1024)S(1)}, f32[768]{0:T(1024)}, u32[]{:S(2)}) copy-start(f32[768]{0:T(1024)} %param.58) | copy-start | bytes 9220
  286.6 11.2 %copy-start.29 = (f32[768]{0:T(1024)S(1)}, f32[768]{0:T(1024)}, u32[]{:S(2)}) copy-start(f32[768]{0:T(1024)} %param.70) | copy-start | bytes 9220
  286.6 12.0 %copy-start.19 = (f32[1024]{0:T(1024)S(1)}, f32[1024]{0:T(1024)}, u32[]{:S(2)}) copy-start(f32[1024]{0:T(1024)} %param.50) | copy-start | bytes 12292
  286.6 12.0 %copy-start.30 = (f32[1024]{0:T(1024)S(1)}, f32[1024]{0:T(1024)}, u32[]{:S(2)}) copy-start(f32[1024]{0:T(1024)} %param.62) | copy-start | bytes 12292
  286.7 12.0 %copy-start.31 = (f32[1024]{0:T(1024)S(1)}, f32[1024]{0:T(1024)}, u32[]{:S(2)}) copy-start(f32[1024]{0:T(1024)} %param.74) | copy-start | bytes 12292
  286.7 12.6 %copy-start.38 = (f32[256]{0:T(256)S(1)}, f32[256]{0:T(256)}, u32[]{:S(2)}) copy-start(f32[256]{0:T(256)} %param.53) | copy-start | bytes 3076
  286.7 12.6 %copy-start.39 = (f32[256]{0:T(256)S(1)}, f32[256]{0:T(256)}, u32[]{:S(2)}) copy-start(f32[256]{0:T(256)} %param.65) | copy-start | bytes 3076
  292.5 7.9 %copy-start.15 = (bf16[512,1024]{1,0:T(8,128)(2,1)S(1)}, bf16[512,1024]{1,0:T(8,128)(2,1)}, u32[]{:S(2)}) copy-start(bf16[512,1024]{1,0:T(8,128)(2,1)} %get-tuple-element.314) | copy-start | bytes 3145732
  292.5 8.9 %copy-start.14 = (bf16[512,1024]{1,0:T(8,128)(2,1)S(1)}, bf16[512,1024]{1,0:T(8,128)(2,1)}, u32[]{:S(2)}) copy-start(bf16[512,1024]{1,0:T(8,128)(2,1)} %get-tuple-element.315) | copy-start | bytes 3145732
  (12 other events, 59.8 us)
